TPU v7x, 32 devices: a whole 2x2x4 slice. The times are simulated.
32 devices in a mesh: gz: 8 (over z, x), col: 4 (over y, core).
Axes of the slice: x: 2, y: 2, z: 4, core: 2. Of those that a mesh axis runs over, the one named last changes fastest.
Arguments:
- features: bfloat16 [64, 16, 128, 128], P(None, 'gz'), may hold values from -6 to 6
- grad_out: bfloat16 [64, 16, 128, 128], P('col', 'gz'), may hold values from -6 to 6
- conv_weight: bfloat16 [64, 64, 27], P('col'), may hold values from -0.15625 to 0.15625
- spectral_weight: bfloat16 [64, 64, 16, 256], P(None, 'col', None, 'gz'), may hold values from -3 to 3
Outputs:
- layer_out: bfloat16 [64, 16, 128, 128], P('col', 'gz')
- grad_input: bfloat16 [64, 16, 128, 128], P('col', 'gz')
- grad_conv: float32 [64, 64, 27], P('col')
- grad_spectral: float32 [64, 64, 16, 256], P(None, 'col', None, 'gz')
All inputs are finite; a program needn't handle non-finite values.
Results may differ from a plain program's by a relative error of at most 0.008.
Values may be sent and summed in bfloat16 or wider, within the bound.
A program may use at most 256 MiB of HBM per device.

v0:
```python
from functools import partial
import math

import jax
import jax.numpy as jnp
from jax import lax
from jax.sharding import PartitionSpec as P

highest = lax.Precision.HIGHEST


def with_halo(block, sides, width):
    for axis, dim in sides:
        count = lax.axis_size(axis)
        forward = [(i, i + 1) for i in range(count - 1)]
        forward.append((count - 1, 0))
        backward = [(target, source) for source, target in forward]
        low = lax.ppermute(
            lax.slice_in_dim(block, block.shape[dim] - width, None, axis=dim), axis, forward
        )
        high = lax.ppermute(lax.slice_in_dim(block, 0, width, axis=dim), axis, backward)
        block = jnp.concatenate([low, block, high], axis=dim)
    return block


def basis(length, mode_count):
    indices = jnp.arange(mode_count, dtype=jnp.int32)
    middle = mode_count // 2
    cosine_rows = indices <= middle
    frequency = jnp.where(cosine_rows, indices, indices - middle)
    positions = jnp.arange(length, dtype=jnp.int32)
    residue = frequency[:, None] * positions[None, :] % length
    radians = residue.astype(jnp.float32) * (2.0 * math.pi / length)
    tables = jnp.where(cosine_rows[:, None], jnp.cos(radians), jnp.sin(radians))
    return tables * math.sqrt(2.0 / length)


def activate(preact, cotangent):
    outcome, pullback = jax.vjp(partial(jax.nn.gelu, approximate=True), preact)
    return (outcome, pullback(cotangent)[0])


def wrap_pad(volume):
    return jnp.pad(volume, ((0, 0), (0, 0), (1, 1), (1, 1)), mode="wrap")


def correlate(padded, kernel):
    numbers = ("NCDHW", "OIDHW", "NCDHW")
    return lax.conv_general_dilated(
        padded[None],
        kernel,
        (1, 1, 1),
        "VALID",
        dimension_numbers=numbers,
        preferred_element_type=jnp.float32,
    )[0]


def analyse(volume, table_x, table_y, table_z):
    channel_count, plane_count, size_x, size_y = volume.shape
    mode_count = table_y.shape[0]
    along_y = jnp.dot(
        volume.reshape(channel_count * plane_count * size_x, size_y),
        table_y.astype(jnp.bfloat16).T,
        preferred_element_type=jnp.float32,
    )
    along_y = along_y.reshape(channel_count, plane_count, size_x, mode_count)
    planes = jnp.einsum("kx,czxl->czkl", table_x, along_y, precision=highest)
    planes = planes.reshape(channel_count, plane_count, mode_count * mode_count)
    return jnp.einsum(
        "jz,czm->cjm",
        table_z,
        lax.all_to_all(planes, "gz", split_axis=2, concat_axis=1, tiled=True),
        precision=highest,
    )


def synthesise(spectrum, table_x, table_y, table_z):
    mode_count = table_x.shape[0]
    columns = jnp.einsum("jz,cjm->czm", table_z, spectrum, precision=highest)
    slabs = lax.all_to_all(columns, "gz", split_axis=1, concat_axis=2, tiled=True)
    channel_count, plane_count, merged = slabs.shape
    blocks = slabs.reshape(channel_count, plane_count, mode_count, mode_count)
    along_x = jnp.einsum("kx,czkl->czxl", table_x, blocks, precision=highest)
    return jnp.einsum("czxl,ly->czxy", along_x, table_y, precision=highest)


def local(features, grad_out, conv_weight, spectral_weight):
    channel_count, plane_count, size_x, size_y = features.shape
    share_count = conv_weight.shape[0]
    mode_count = spectral_weight.shape[2]
    groups = lax.axis_size("gz")
    table_x = basis(size_x, mode_count)
    table_y = basis(size_y, mode_count)
    table_z = basis(plane_count * groups, mode_count)
    first_channel = lax.axis_index("col") * share_count
    own_features = lax.dynamic_slice_in_dim(features, first_channel, share_count, 0)
    rimmed = with_halo(features, (("gz", 1),), 1)
    padded = wrap_pad(rimmed)
    kernel = conv_weight.reshape(share_count, channel_count, 3, 3, 3)
    conv_part = correlate(padded, kernel)
    weights32 = spectral_weight.astype(jnp.float32)
    spectrum = analyse(own_features, table_x, table_y, table_z)
    spectrum_all = lax.all_gather(spectrum, "col", axis=0, tiled=True)
    mixed = jnp.sum(weights32 * spectrum_all[:, None], axis=0)
    preact = conv_part + synthesise(mixed, table_x, table_y, table_z)
    outcome, slope = activate(preact, grad_out.astype(jnp.float32))
    layer_out = outcome.astype(jnp.bfloat16)
    grad_pre = slope.astype(jnp.bfloat16)
    grad_framed = with_halo(grad_pre, (("gz", 1),), 1)
    flipped = jnp.transpose(kernel, (1, 0, 2, 3, 4))[:, :, ::-1, ::-1, ::-1]
    contributions = correlate(wrap_pad(grad_framed), flipped)
    back_conv = lax.psum_scatter(contributions, "col", scatter_dimension=0, tiled=True)
    numbers = ("NCDHW", "OIDHW", "NCDHW")
    local_grad = lax.conv_general_dilated(
        padded[:, None],
        grad_pre[:, None],
        (1, 1, 1),
        "VALID",
        dimension_numbers=numbers,
        preferred_element_type=jnp.float32,
    )
    local_grad = jnp.transpose(local_grad, (1, 0, 2, 3, 4)).reshape(share_count, channel_count, 27)
    scaling = 1.0 / math.sqrt(size_x * size_y * plane_count * groups)
    grad_conv = lax.psum(local_grad, "gz") * scaling
    grad_modes = analyse(grad_pre, table_x, table_y, table_z)
    back_terms = jnp.sum(weights32 * grad_modes[None], axis=1)
    back_modes = lax.psum_scatter(
        back_terms.astype(jnp.bfloat16), "col", scatter_dimension=0, tiled=True
    ).astype(jnp.float32)
    grad_input = (back_conv + synthesise(back_modes, table_x, table_y, table_z)).astype(
        jnp.bfloat16
    )
    grad_spectral = spectrum_all[:, None] * grad_modes[None]
    return (layer_out, grad_input, grad_conv, grad_spectral)


def solution(mesh):
    return jax.shard_map(
        local,
        mesh=mesh,
        in_specs=(
            P(None, "gz", None, None),
            P("col", "gz", None, None),
            P("col", None, None),
            P(None, "col", None, "gz"),
        ),
        out_specs=(
            P("col", "gz", None, None),
            P("col", "gz", None, None),
            P("col", None, None),
            P(None, "col", None, "gz"),
        ),
        check_vma=False,
    )
```

profile of v0, /device:TPU:0, one launch (start us, length us, event | category | flops | bytes accessed | tf_op | source)
XLA Modules:
  0.0 921.5 jit_solution(8178121474838906270)
XLA Ops:
  8.0 6.5 copy.109
  28.6 85.3 %all_to_all.66 = f32[8,1,1024]{2,1,0:T(1,128)S(1)} all-to-all(f32[8,1,1024]{2,1,0:T(1,128)S(1)} %reshape.84), channel_id=1, replica_groups=mesh['gz'=8,'col'=4] {'gz'}, dimensions={0} | all-to-all | bytes 65536 | tf_op jit(solution)/shard_map/all_to_all | solution.py:73
  116.1 7.2 all_gather.3
  127.0 13.1 %all_to_all.67 = f32[8,1,1024]{2,1,0:T(1,128)S(1)} all-to-all(f32[8,1,1024]{2,1,0:T(1,128)S(1)} %reshape.86), channel_id=1, replica_groups=mesh['gz'=8,'col'=4] {'gz'}, dimensions={0} | all-to-all | bytes 65536 | tf_op jit(solution)/shard_map/all_to_all | solution.py:81
  145.5 7.1 fusion.132
  152.6 42.4 %fusion.153 = bf16[64,4,130,1,130]{2,0,4,1,3:T(8,128)(2,1)} fusion(bf16[64,4,1,128]{2,0,3,1:T(8,128)(2,1)} %get-tuple-element.5, bf16[64,1,128,128]{2,0,3,1:T(8,128)(2,1)S(1)} %collective-permute-done.1, bf16[64,2,128,128]{2,0,3,1:T(8,128)(2,1)} %copy.109, bf16[64,1,128,128]{2,0,3,1:T(8,128)(2,1)} %collective-permute-done, ...), kind=kLoop, calls=%fused_computation.181 | loop fusion | flops 129792000 | bytes 17172480 | tf_op jit(solution)/shard_map/broadcast_in_dim | solution.py:50
  195.0 15.7 %pad = bf16[64,4,130,1,136]{2,0,4,1,3:T(8,128)(2,1)} pad(bf16[64,4,130,1,130]{2,0,4,1,3:T(8,128)(2,1)} %fusion.153, bf16[]{:T(256)} %constant.69), padding=0_0x0_0x0_0x0_0x0_6 | pad | bytes 17704962 | tf_op jit(solution)/shard_map/broadcast_in_dim | solution.py:50
  210.7 29.9 %copy.113 = bf16[64,4,130,1,8,17]{0,4,5,2,1,3:T(8,128)(2,1)} copy(bf16[64,4,130,1,8,17]{2,0,5,4,1,3:T(8,128)(2,1)} %bitcast.133) | data formatting | bytes 18104320 | tf_op jit(solution)/shard_map/conv_general_dilated | solution.py:49
  242.8 71.5 %broadcast_select_fusion.1 = f32[2,128,8,17,16]{4,2,3,1,0:T(8,128)} fusion(pred[8,17]{0,1:T(8,128)(4,1)S(1)} %copy-done.8, bf16[16,64,3,3,3]{1,0,4,3,2:T(8,128)(2,1)S(1)} %bitcast.131, bf16[64,4,130,1,7,2]{0,4,5,2,1,3:T(8,128)(2,1)S(1)} %slice.64, bf16[64,4,130,1,8,17]{0,4,5,2,1,3:T(8,128)(2,1)} %copy.113), kind=kOutput, calls=%fused_computation.29 | convolution fusion | flops 1956093952 | bytes 12267656 | tf_op jit(solution)/shard_map/conv_general_dilated | solution.py:49
  314.3 11.9 %copy.114 = f32[2,128,8,17,16]{1,4,3,2,0:T(8,128)} copy(f32[2,128,8,17,16]{4,2,3,1,0:T(8,128)} %broadcast_select_fusion.1) | data formatting | bytes 4456448 | tf_op jit(solution)/shard_map/conv_general_dilated | solution.py:49
  332.1 7.0 fusion.28
  350.8 42.4 %fusion.152 = bf16[64,1,4,130,130]{3,0,4,2,1:T(8,128)(2,1)} fusion(bf16[64,4,1,128]{2,0,3,1:T(8,128)(2,1)} %get-tuple-element.5, bf16[64,1,128,128]{2,0,3,1:T(8,128)(2,1)S(1)} %collective-permute-done.1, bf16[64,2,128,128]{2,0,3,1:T(8,128)(2,1)} %copy.109, bf16[64,1,128,128]{2,0,3,1:T(8,128)(2,1)} %collective-permute-done, ...), kind=kLoop, calls=%fused_computation.180 | loop fusion | flops 129792000 | bytes 17172480 | tf_op jit(solution)/shard_map/broadcast_in_dim | solution.py:116
  393.3 71.1 %copy.140 = bf16[64,1,4,130,130]{0,1,4,3,2:T(2,128)(2,1)} copy(bf16[64,1,4,130,130]{3,0,4,2,1:T(8,128)(2,1)} %fusion.152) | data formatting | bytes 17305600 | tf_op jit(solution)/shard_map/broadcast_in_dim | solution.py:116
  464.3 17.8 %copy.141 = bf16[16,1,2,128,128]{0,1,4,3,2:T(2,128)(2,1)} copy(bf16[16,1,2,128,128]{4,3,2,0,1:T(8,128)(2,1)S(1)} %bitcast.134) | data formatting | bytes 2097152 | tf_op jit(solution)/shard_map/broadcast_in_dim | solution.py:117
  493.6 233.9 %fusion.136 = f32[16,64,3,3,3]{1,0,4,3,2:T(8,128)} fusion(bf16[64,1,4,130,130]{0,1,4,3,2:T(2,128)(2,1)} %copy.140, bf16[16,1,2,128,128]{0,1,4,3,2:T(2,128)(2,1)} %copy.141), kind=kOutput, calls=%fused_computation.179 | convolution fusion | flops 1811939328 | bytes 9811968 | tf_op jit(solution)/shard_map/transpose | solution.py:123
  731.7 7.7 maximum_bitcast_fusion
  739.4 8.3 copy.160
  752.8 18.3 %copy.127 = bf16[16,4,130,1,8,17]{0,4,5,2,1,3:T(8,128)(2,1)} copy(bf16[16,4,130,1,8,17]{2,0,5,4,1,3:T(8,128)(2,1)} %bitcast.137) | data formatting | bytes 4526080 | tf_op jit(solution)/shard_map/conv_general_dilated | solution.py:49
  773.3 29.9 %broadcast_select_fusion = f32[2,128,8,17,64]{4,2,3,1,0:T(8,128)} fusion(pred[8,17]{0,1:T(8,128)(4,1)S(1)} %copy-done.9, bf16[16,64,3,3,3]{1,0,4,3,2:T(8,128)(2,1)S(1)} %bitcast.132, bf16[16,4,130,1,7,2]{0,4,5,2,1,3:T(8,128)(2,1)S(1)} %slice.70, bf16[16,4,130,1,8,17]{0,4,5,2,1,3:T(8,128)(2,1)} %copy.127), kind=kOutput, calls=%fused_computation.28 | convolution fusion | flops 1935001600 | bytes 11464328 | tf_op jit(solution)/shard_map/conv_general_dilated | solution.py:49
  803.2 14.9 %copy.128 = f32[2,128,8,17,64]{1,4,3,2,0:T(8,128)} copy(f32[2,128,8,17,64]{4,2,3,1,0:T(8,128)} %broadcast_select_fusion) | data formatting | bytes 17825792 | tf_op jit(solution)/shard_map/conv_general_dilated | solution.py:49
  818.0 8.3 slice.71
  826.3 9.2 copy.159
  837.5 6.3 all-to-all-start.3
  852.0 55.8 %reduce-scatter.3.cloned.1.call-done = f32[16,2,128,128]{3,2,1,0:T(8,128)} async-done(((f32[64,2,128,128]{3,2,1,0:T(8,128)}), f32[16,2,128,128]{3,2,1,0:T(8,128)}) %reduce-scatter.3.cloned.1.call-update) | async-done | bytes 2097168 | tf_op jit(solution)/shard_map/reduce_scatter | solution.py:113
  (93 shorter events, 83.7 us)
Async XLA Ops:
  8.0 234.8 %copy-start = (bf16[16,64,27]{1,0,2:T(8,128)(2,1)S(1)}, bf16[16,64,27]{1,0,2:T(8,128)(2,1)}, u32[]{:S(2)}) copy-start(bf16[16,64,27]{1,0,2:T(8,128)(2,1)} %param.6) | copy-start | bytes 165892
  19.6 122.1 %collective-permute-start.1 = (bf16[64,1,128,128]{2,0,3,1:T(8,128)(2,1)}, bf16[64,1,128,128]{2,0,3,1:T(8,128)(2,1)S(1)}, u32[]{:S(2)}, u32[]{:S(2)}) collective-permute-start(bf16[64,1,128,128]{2,0,3,1:T(8,128)(2,1)} %get-tuple-element.7), channel_id=1, source_target_pairs={{4,0},{8,4},{12,8},{16,12},{20,16},{24,20},{28,24},{0,28},{5,1},{9... | collective-permute-start | bytes 6291464 | tf_op jit(solution)/shard_map/ppermute | solution.py:21
  25.6 116.1 %collective-permute-start = (bf16[64,1,128,128]{2,0,3,1:T(8,128)(2,1)}, bf16[64,1,128,128]{2,0,3,1:T(8,128)(2,1)}, u32[]{:S(2)}, u32[]{:S(2)}) collective-permute-start(bf16[64,1,128,128]{2,0,3,1:T(8,128)(2,1)} %get-tuple-element.6), channel_id=1, source_target_pairs={{0,4},{4,8},{8,12},{12,16},{16,20},{20,24},{24,28},{28,0},{1,5},{5... | collective-permute-start | bytes 6291464 | tf_op jit(solution)/shard_map/ppermute | solution.py:18
  25.6 461.7 %copy-start.4 = (s32[16]{0:T(128)}, s32[16]{0:T(128)S(1)}, u32[]{:S(2)}) copy-start(s32[16]{0:T(128)S(1)} %add_select_fusion.2) | copy-start | bytes 196
  25.7 317.1 %copy-start.6 = (pred[16]{0:T(512)(128)(4,1)}, pred[16]{0:T(512)(128)(4,1)S(1)}, u32[]{:S(2)}) copy-start(pred[16]{0:T(512)(128)(4,1)S(1)} %iota_compare_fusion.2) | copy-start | bytes 52
  123.6 21.9 %copy-start.2 = (f32[64,16,32]{0,2,1:T(8,128)}, f32[64,16,32]{0,2,1:T(8,128)S(1)}, u32[]{:S(2)}) copy-start(f32[64,16,32]{0,2,1:T(8,128)S(1)} %copy.121) | copy-start | bytes 393220
  210.7 32.1 %copy-start.8 = (pred[8,17]{0,1:T(8,128)(4,1)S(1)}, pred[8,17]{0,1:T(8,128)(4,1)}, u32[]{:S(2)}) copy-start(pred[8,17]{0,1:T(8,128)(4,1)} %constant.77) | copy-start | bytes 412
  340.7 386.9 %collective-permute-start.3 = (bf16[16,1,128,128]{3,2,1,0:T(8,128)(2,1)}, bf16[16,1,128,128]{3,2,1,0:T(8,128)(2,1)}, u32[]{:S(2)}, u32[]{:S(2)}) collective-permute-start(bf16[16,1,128,128]{3,2,1,0:T(8,128)(2,1)} %get-tuple-element.15), channel_id=1, source_target_pairs={{4,0},{8,4},{12,8},{16,12},{20,16},{24,20},{28,24},{0,28},{5,1},{9... | collective-permute-start | bytes 1572872 | tf_op jit(solution)/shard_map/ppermute | solution.py:21
  341.4 386.2 %collective-permute-start.2 = (bf16[16,1,128,128]{3,2,1,0:T(8,128)(2,1)}, bf16[16,1,128,128]{3,2,1,0:T(8,128)(2,1)}, u32[]{:S(2)}, u32[]{:S(2)}) collective-permute-start(bf16[16,1,128,128]{3,2,1,0:T(8,128)(2,1)} %get-tuple-element.14), channel_id=1, source_target_pairs={{0,4},{4,8},{8,12},{12,16},{16,20},{20,24},{24,28},{28,0},{1,5},{5... | collective-permute-start | bytes 1572872 | tf_op jit(solution)/shard_map/ppermute | solution.py:18
  346.1 135.9 %all-to-all-start.2 = ((f32[8,1,1024]{2,1,0:T(1,128)}), f32[8,1,1024]{2,1,0:T(1,128)}, u32[]{:S(2)}, u32[]{:S(2)}) async-start(f32[8,1,1024]{2,1,0:T(1,128)} %reshape.88), calls=%async_computation.3 | async-start | bytes 65536 | tf_op jit(solution)/shard_map/all_to_all | solution.py:73
  350.8 484.8 %reduce-scatter.5.cloned.1.call-start = ((), (), s32[]{:S(2)}) async-start(), calls=%async_computation.7 | async-start | bytes 327680 | tf_op jit(solution)/shard_map/reduce_scatter | solution.py:128
  464.3 24.0 %copy-start.1 = (bf16[64,16,16,32]{0,3,2,1:T(8,128)(2,1)S(1)}, bf16[64,16,16,32]{0,3,2,1:T(8,128)(2,1)}, u32[]{:S(2)}) copy-start(bf16[64,16,16,32]{0,3,2,1:T(8,128)(2,1)} %param.7) | copy-start | bytes 3145732
  464.3 24.0 %copy-start.3 = (f32[64,16,32]{0,2,1:T(8,128)S(1)}, f32[64,16,32]{0,2,1:T(8,128)}, u32[]{:S(2)}) copy-start(f32[64,16,32]{0,2,1:T(8,128)} %copy-done.2) | copy-start | bytes 393220
  493.5 350.3 %all-reduce.2.cloned.1.call-start = ((), (), s32[]{:S(2)}) async-start(), calls=%async_computation.8 | async-start | bytes 442368 | tf_op jit(solution)/shard_map/psum | solution.py:125
  727.5 180.3 %reduce-scatter.3.cloned.1.call-start = ((), (), s32[]{:S(2)}) async-start(), calls=%async_computation.6 | async-start | bytes 10485760 | tf_op jit(solution)/shard_map/reduce_scatter | solution.py:113
  752.8 20.5 %copy-start.9 = (pred[8,17]{0,1:T(8,128)(4,1)S(1)}, pred[8,17]{0,1:T(8,128)(4,1)}, u32[]{:S(2)}) copy-start(pred[8,17]{0,1:T(8,128)(4,1)} %constant.77) | copy-start | bytes 412
  826.3 9.3 %copy-start.5 = (s32[16]{0:T(128)S(1)}, s32[16]{0:T(128)}, u32[]{:S(2)}) copy-start(s32[16]{0:T(128)} %copy-done.4) | copy-start | bytes 196
  826.3 9.3 %copy-start.7 = (pred[16]{0:T(512)(128)(4,1)S(1)}, pred[16]{0:T(512)(128)(4,1)}, u32[]{:S(2)}) copy-start(pred[16]{0:T(512)(128)(4,1)} %copy-done.6) | copy-start | bytes 52
  837.5 12.9 %all-to-all-start.3 = ((f32[8,1,1024]{2,1,0:T(1,128)}), f32[8,1,1024]{2,1,0:T(1,128)S(1)}, u32[]{:S(2)}, u32[]{:S(2)}) async-start(f32[8,1,1024]{2,1,0:T(1,128)} %reshape.90), calls=%async_computation.5 | async-start | bytes 65536 | tf_op jit(solution)/shard_map/all_to_all | solution.py:81
Sparse Core Ops, SparseCore 0:
  493.7 20.7 reduce-scatter.4
  835.7 72.1 reduce-scatter.2
Sparse Core Ops, SparseCore 1:
  727.6 71.2 all-reduce.1
where the time goes:
time: 931 us; the launch traced here: 921 us
  matrix products  355 us (38%)
  local copies, waits for them, and re-layouts  253 us (27%)
  other arithmetic  111 us (12%)
  blocking collectives  106 us (11%)
  waiting for transfers between devices  60.9 us (7%)
  starting transfers between devices  19.1 us (2%)
  between operations  16.4 us (2%)
    transpose x1, matrix products, local(): jnp.transpose(local_grad, (1, 0, 2, 3, 4))  234 us
    conv_general_dilated x2, matrix products, correlate(): lax.conv_general_dilated(padded[None], kernel, (1, 1, 1), 'VALID', dimens...  101 us
    conv_general_dilated x8, local copies, waits for them, and re-layouts, correlate(): lax.conv_general_dilated(padded[None], kernel, (1, 1, 1), 'VALID', dimens...  90.6 us
    all_to_all x1, blocking collectives, analyse(): lax.all_to_all(planes, 'gz', split_axis=2, concat_axis=1, tiled=True)  85.3 us
    broadcast_in_dim x1, local copies, waits for them, and re-layouts, local(): padded[:, None]  71.1 us
    reduce_scatter x1, waiting for transfers between devices, local(): lax.psum_scatter(contributions, 'col', scatter_dimension=0, tiled=True)  55.8 us
    broadcast_in_dim x2, other arithmetic, correlate(): padded[None]  50.1 us
    broadcast_in_dim x1, other arithmetic, local(): padded[:, None]  42.4 us
  transfers between devices with their start and end apart: 9, of which 2 were waited for; matrix products, arithmetic and copies ran while one was open for 55% of the time, Pallas kernels for 0%

commit v1 on v0

v1 whole, which is shorter than its diff:
```python
from functools import partial
import math

import jax
import jax.numpy as jnp
import numpy as np
from jax import lax
from jax.experimental import pallas as pl
from jax.experimental.pallas import tpu as pltpu
from jax.sharding import PartitionSpec as P

highest = lax.Precision.HIGHEST
f32 = jnp.float32
bf16 = jnp.bfloat16


def basis(length, mode_count):
    indices = np.arange(mode_count)
    middle = mode_count // 2
    cosine_rows = indices <= middle
    frequency = np.where(cosine_rows, indices, indices - middle)
    residue = frequency[:, None] * np.arange(length)[None, :] % length
    radians = residue * (2.0 * math.pi / length)
    tables = np.where(cosine_rows[:, None], np.cos(radians), np.sin(radians))
    return (tables * math.sqrt(2.0 / length)).astype(np.float32)


def split_table(table):
    high = table.astype(bf16)
    return high, (table - high.astype(np.float32)).astype(bf16)


def neighbours(axis):
    count = lax.axis_size(axis)
    up = [(i, (i + 1) % count) for i in range(count)]
    down = [((i + 1) % count, i) for i in range(count)]
    return up, down


def params(*semantics):
    return pltpu.CompilerParams(
        dimension_semantics=semantics, vmem_limit_bytes=48 * 1024 * 1024
    )


def slab_modes(slab_of, count, ex2, eyt):
    modes = ex2.shape[0] // 2
    parts = []
    for s in range(count):
        both = jnp.dot(ex2, slab_of(s), preferred_element_type=f32)
        parts.append(both[:modes] + both[modes:])
    along_x = jnp.concatenate(parts, axis=0)
    high = along_x.astype(bf16)
    low = (along_x - high.astype(f32)).astype(bf16)
    return jnp.dot(high, eyt, preferred_element_type=f32) + jnp.dot(
        low, eyt, preferred_element_type=f32
    )


def analyse_kernel(v_ref, ex_ref, ey_ref, o_ref):
    count = v_ref.shape[0]
    ex2, eyt = ex_ref[...], ey_ref[...]
    out = slab_modes(lambda s: v_ref[s], count, ex2, eyt)
    o_ref[...] = out.reshape(o_ref.shape)


def analyse_slabs(volume, ex2, eyt):
    slabs, size_x, size_y = volume.shape
    modes = eyt.shape[1]
    block = 16
    return pl.pallas_call(
        analyse_kernel,
        grid=(slabs // block,),
        in_specs=[
            pl.BlockSpec((block, size_x, size_y), lambda g: (g, 0, 0)),
            pl.BlockSpec(ex2.shape, lambda g: (0, 0)),
            pl.BlockSpec(eyt.shape, lambda g: (0, 0)),
        ],
        out_specs=pl.BlockSpec((block, modes, modes), lambda g: (g, 0, 0)),
        out_shape=jax.ShapeDtypeStruct((slabs, modes, modes), f32),
        compiler_params=params("arbitrary"),
        name="analyse",
    )(volume, ex2, eyt)


def conv_kernel(rows, size_y, f_ref, w_ref, o_ref):
    start = pl.program_id(0) * rows * size_y
    total = None
    depth = f_ref.shape[0]
    span = rows * size_y
    for b in range(3):
        first = pl.multiple_of(start + b * size_y, size_y)
        part = jnp.dot(
            w_ref[:, b * depth : (b + 1) * depth],
            f_ref[:, pl.ds(first, span)],
            preferred_element_type=f32,
        )
        total = part if total is None else total + part
    count = total.shape[0] // 3
    flat = o_ref.reshape(count * rows, size_y)
    for r in range(rows):
        piece = total[:, r * size_y : (r + 1) * size_y]
        value = (
            pltpu.roll(piece[:count], 1, 1)
            + piece[count : 2 * count]
            + pltpu.roll(piece[2 * count :], size_y - 1, 1)
        )
        flat[pl.ds(r, count, stride=rows), :] = value


def forward_conv(framed, weights, size_x, size_y):
    count = weights.shape[0] // 3
    rows = 8
    return pl.pallas_call(
        partial(conv_kernel, rows, size_y),
        grid=(size_x // rows,),
        in_specs=[
            pl.BlockSpec(framed.shape, lambda g: (0, 0)),
            pl.BlockSpec(weights.shape, lambda g: (0, 0)),
        ],
        out_specs=pl.BlockSpec((count, rows, size_y), lambda g: (0, g, 0)),
        out_shape=jax.ShapeDtypeStruct((count, size_x, size_y), f32),
        compiler_params=params("arbitrary"),
        name="forward_conv",
    )(framed, weights)


def planar(spectrum, ext, ey):
    along_x = jnp.dot(ext, spectrum, precision=highest, preferred_element_type=f32)
    return jnp.dot(along_x, ey, precision=highest, preferred_element_type=f32)


def gelu_kernel(c_ref, lo_ref, hi_ref, s_ref, g_ref, ext_ref, ey_ref, ex2_ref, eyt_ref,
                out_ref, gp_ref, m_ref):
    plane = pl.program_id(0)
    last = pl.num_programs(0) - 1
    count = c_ref.shape[1]
    keep_lo = jnp.where(plane == 0, 1.0, 0.0).astype(f32)
    keep_hi = jnp.where(plane == last, 1.0, 0.0).astype(f32)
    ext, ey = ext_ref[...], ey_ref[...]
    k0 = math.sqrt(2.0 / math.pi)
    k1 = 0.044715
    for o in range(count):
        v = c_ref[0, o] + lo_ref[o].astype(f32) * keep_lo + hi_ref[o].astype(f32) * keep_hi
        v = v + planar(s_ref[0, o], ext, ey)
        v2 = v * v
        t = jnp.tanh(k0 * v * (1.0 + k1 * v2))
        half = 0.5 * (1.0 + t)
        out_ref[o, 0] = (v * half).astype(bf16)
        slope = half + (0.5 * k0) * v * (1.0 - t * t) * (1.0 + (3.0 * k1) * v2)
        gp_ref[o, 0] = (g_ref[o, 0].astype(f32) * slope).astype(bf16)
    modes = slab_modes(lambda o: gp_ref[o, 0], count, ex2_ref[...], eyt_ref[...])
    m_ref[...] = modes.reshape(m_ref.shape)


def gelu_stage(conv, low, high, slabs, grad_out, tables):
    ext, ey, ex2, eyt = tables
    share, planes, size_x, size_y = grad_out.shape
    modes = ey.shape[0]
    block = 8
    field = pl.BlockSpec((block, 1, size_x, size_y), lambda z, g: (g, z, 0, 0))
    rim = pl.BlockSpec((block, size_x, size_y), lambda z, g: (g, 0, 0))
    whole = lambda t: pl.BlockSpec(t.shape, lambda z, g: (0, 0))
    return pl.pallas_call(
        gelu_kernel,
        grid=(planes, share // block),
        in_specs=[
            pl.BlockSpec((1, block, size_x, size_y), lambda z, g: (z + 1, g, 0, 0)),
            rim,
            rim,
            pl.BlockSpec((1, block, modes, modes), lambda z, g: (z, g, 0, 0)),
            field,
            whole(ext),
            whole(ey),
            whole(ex2),
            whole(eyt),
        ],
        out_specs=[
            field,
            field,
            pl.BlockSpec((1, block, modes, modes), lambda z, g: (z, g, 0, 0)),
        ],
        out_shape=[
            jax.ShapeDtypeStruct(grad_out.shape, bf16),
            jax.ShapeDtypeStruct(grad_out.shape, bf16),
            jax.ShapeDtypeStruct((planes, share, modes, modes), f32),
        ],
        compiler_params=params("arbitrary", "arbitrary"),
        name="gelu_stage",
    )(conv, low, high, slabs, grad_out, ext, ey, ex2, eyt)


def back_kernel(rows, size_y, g_ref, f_ref, w_ref, c_ref, acc_ref, roll_ref):
    step = pl.program_id(0)
    height = g_ref.shape[0]
    span = rows * size_y

    @pl.when(step == 0)
    def _():
        acc_ref[...] = jnp.zeros_like(acc_ref)

        def shift(r, carry):
            lanes = pl.ds(pl.multiple_of(r * size_y, size_y), size_y)
            block = g_ref[:, lanes]
            wide = block.astype(f32)
            roll_ref[:height, lanes] = pltpu.roll(wide, size_y - 1, 1).astype(bf16)
            roll_ref[height : 2 * height, lanes] = block
            roll_ref[2 * height :, lanes] = pltpu.roll(wide, 1, 1).astype(bf16)
            return carry

        lax.fori_loop(0, g_ref.shape[1] // size_y, shift, 0)

    start = step * span
    shifted = []
    for b in range(3):
        first = pl.multiple_of(start + (2 - b) * size_y, size_y)
        shifted.append(roll_ref[:, pl.ds(first, span)])
    stacked = jnp.concatenate(shifted, axis=0)
    c_ref[...] = jnp.dot(w_ref[...], stacked, preferred_element_type=f32).astype(bf16)
    acc_ref[...] += lax.dot_general(
        stacked, f_ref[...], (((1,), (1,)), ((), ())), preferred_element_type=f32
    )


def backward_convs(grad_framed, framed, weights, size_x, size_y):
    height = grad_framed.shape[0]
    depth = framed.shape[0]
    rows = 8
    span = rows * size_y
    return pl.pallas_call(
        partial(back_kernel, rows, size_y),
        grid=(size_x // rows,),
        in_specs=[
            pl.BlockSpec(grad_framed.shape, lambda g: (0, 0)),
            pl.BlockSpec((depth, span), lambda g: (0, g)),
            pl.BlockSpec(weights.shape, lambda g: (0, 0)),
        ],
        out_specs=[
            pl.BlockSpec((depth, span), lambda g: (0, g)),
            pl.BlockSpec((9 * height, depth), lambda g: (0, 0)),
        ],
        out_shape=[
            jax.ShapeDtypeStruct((depth, size_x * size_y), bf16),
            jax.ShapeDtypeStruct((9 * height, depth), f32),
        ],
        scratch_shapes=[pltpu.VMEM((3 * height, grad_framed.shape[1]), bf16)],
        compiler_params=params("arbitrary"),
        name="backward_convs",
    )(grad_framed, framed, weights)


def final_kernel(a_ref, b_ref, s_ref, ext_ref, ey_ref, o_ref):
    ext, ey = ext_ref[...], ey_ref[...]
    for i in range(a_ref.shape[0]):
        total = a_ref[i].astype(f32) + b_ref[i].astype(f32) + planar(s_ref[i], ext, ey)
        o_ref[i] = total.astype(bf16)


def final_stage(own, other, slabs, tables):
    ext, ey = tables[:2]
    count, size_x, size_y = own.shape
    modes = ey.shape[0]
    block = 8
    field = pl.BlockSpec((block, size_x, size_y), lambda g: (g, 0, 0))
    return pl.pallas_call(
        final_kernel,
        grid=(count // block,),
        in_specs=[
            field,
            field,
            pl.BlockSpec((block, modes, modes), lambda g: (g, 0, 0)),
            pl.BlockSpec(ext.shape, lambda g: (0, 0)),
            pl.BlockSpec(ey.shape, lambda g: (0, 0)),
        ],
        out_specs=field,
        out_shape=jax.ShapeDtypeStruct(own.shape, bf16),
        compiler_params=params("arbitrary"),
        name="final_stage",
    )(own, other, slabs, ext, ey)


def to_modes(planes, table_z):
    gathered = lax.all_to_all(planes, "gz", split_axis=2, concat_axis=1, tiled=True)
    return jnp.einsum("jz,czm->cjm", table_z, gathered, precision=highest)


def to_slabs(spectrum, table_z):
    columns = jnp.einsum("jz,cjm->czm", table_z, spectrum, precision=highest)
    return lax.all_to_all(columns, "gz", split_axis=1, concat_axis=2, tiled=True)


def halve(block, bit):
    count = lax.axis_size("col")
    side = (lax.axis_index("col") // bit) % 2
    pairs = [(i, i ^ bit) for i in range(count)]
    mine = lax.dynamic_index_in_dim(block, side, 0, keepdims=False)
    other = lax.dynamic_index_in_dim(block, 1 - side, 0, keepdims=False)
    return mine, lax.ppermute(other, "col", pairs)


def frame(flat, size_y):
    return jnp.concatenate([flat[:, -size_y:], flat, flat[:, :size_y]], axis=1)


def local(features, grad_out, conv_weight, spectral_weight):
    channels, planes, size_x, size_y = features.shape
    share = conv_weight.shape[0]
    modes = spectral_weight.shape[2]
    groups = lax.axis_size("gz")
    parts = lax.axis_size("col")
    table_x = basis(size_x, modes)
    table_y = basis(size_y, modes)
    table_z = basis(planes * groups, modes)
    ex2 = np.concatenate(split_table(table_x), axis=0)
    eyt = np.ascontiguousarray(table_y.astype(bf16).T)
    tables = tuple(
        jnp.asarray(t) for t in (np.ascontiguousarray(table_x.T), table_y, ex2, eyt)
    )
    table_z = jnp.asarray(table_z)
    up, down = neighbours("gz")

    pick = np.zeros((3, planes, planes + 2), np.float32)
    for z in range(planes):
        for a in range(3):
            pick[a, z, z - a + 2] = 1.0
    kernel = conv_weight.reshape(share, channels, 3, 3, 3)
    spread = jnp.einsum(
        "oiabc,azp->oizpbc", kernel, jnp.asarray(pick, bf16), preferred_element_type=bf16
    )
    w_forward = jnp.transpose(spread, (5, 3, 0, 4, 1, 2)).reshape(
        3 * (planes + 2) * share, 3 * channels * planes
    )
    w_back = jnp.transpose(spread, (1, 2, 4, 5, 0, 3)).reshape(
        channels * planes, 9 * share * (planes + 2)
    )

    first_channel = lax.axis_index("col") * share
    own = lax.dynamic_slice_in_dim(features, first_channel, share, 0)
    planar_modes = analyse_slabs(own.reshape(share * planes, size_x, size_y), *tables[2:])
    spectrum = to_modes(planar_modes.reshape(share, planes, modes * modes), table_z)
    spectrum_all = lax.all_gather(spectrum, "col", axis=0, tiled=True)

    framed = frame(features.reshape(channels * planes, size_x * size_y), size_y)
    conv = forward_conv(framed, w_forward, size_x, size_y)
    conv = conv.reshape(planes + 2, share, size_x, size_y)
    low = lax.ppermute(conv[planes + 1].astype(bf16), "gz", up)
    high = lax.ppermute(conv[0].astype(bf16), "gz", down)

    weights32 = spectral_weight.astype(f32)
    mixed = jnp.sum(weights32 * spectrum_all[:, None], axis=0)
    slabs = to_slabs(mixed, table_z)
    slabs = jnp.transpose(slabs.reshape(share, planes, modes, modes), (1, 0, 2, 3))
    layer_out, grad_pre, grad_planar = gelu_stage(conv, low, high, slabs, grad_out, tables)

    before = lax.ppermute(grad_pre[:, planes - 1 :], "gz", up)
    after = lax.ppermute(grad_pre[:, :1], "gz", down)
    grad_planar = jnp.transpose(grad_planar, (1, 0, 2, 3)).reshape(share, planes, modes * modes)
    grad_modes = to_modes(grad_planar, table_z)

    rimmed = jnp.concatenate([before, grad_pre, after], axis=1)
    grad_framed = frame(rimmed.reshape(share * (planes + 2), size_x * size_y), size_y)
    contributions, products = backward_convs(
        grad_framed, framed[:, size_y:-size_y], w_back, size_x, size_y
    )
    block = contributions.reshape(parts, share * planes, size_x * size_y)
    bit = 1
    received = None
    while bit < parts:
        if received is not None:
            block = (block.astype(f32) + received.astype(f32)).astype(bf16)
        paired = block.reshape(block.shape[0] // 2, 2, *block.shape[1:])
        block, received = halve(jnp.swapaxes(paired, 0, 1), bit)
        bit *= 2
    shape = (share * planes, size_x, size_y)
    block, received = block.reshape(shape), received.reshape(shape)

    products = products.reshape(3, 3, share, planes + 2, channels, planes)
    taps = [
        sum(products[:, :, :, z - a + 2, :, z] for z in range(planes)) for a in range(3)
    ]
    local_grad = jnp.stack(taps, axis=0)
    scaling = 1.0 / math.sqrt(size_x * size_y * planes * groups)
    grad_conv = lax.psum(local_grad.reshape(27 * share, channels), "gz") * scaling
    grad_conv = jnp.transpose(grad_conv.reshape(27, share, channels), (1, 2, 0))

    back_terms = jnp.sum(weights32 * grad_modes[None], axis=1)
    back_modes = lax.psum_scatter(
        back_terms.astype(bf16), "col", scatter_dimension=0, tiled=True
    ).astype(f32)
    back_slabs = to_slabs(back_modes, table_z).reshape(share * planes, modes, modes)
    grad_input = final_stage(block, received, back_slabs, tables)
    grad_input = grad_input.reshape(share, planes, size_x, size_y)
    grad_spectral = spectrum_all[:, None] * grad_modes[None]
    return (layer_out, grad_input, grad_conv, grad_spectral)


def solution(mesh):
    return jax.shard_map(
        local,
        mesh=mesh,
        in_specs=(
            P(None, "gz", None, None),
            P("col", "gz", None, None),
            P("col", None, None),
            P(None, "col", None, "gz"),
        ),
        out_specs=(
            P("col", "gz", None, None),
            P("col", "gz", None, None),
            P("col", None, None),
            P(None, "col", None, "gz"),
        ),
        check_vma=False,
    )
```

time: 931 us -> 274 us (0.29)
  matrix products: 355 us -> 2 us
  local copies, waits for them, and re-layouts: 253 us -> 55.7 us
  other arithmetic: 111 us -> 28.1 us
  blocking collectives: 106 us -> 26.1 us
  Pallas kernels: 0 us -> 50.7 us
  waiting for transfers between devices: 60.9 us -> 71.2 us
    transpose x1 -> x0, matrix products: 234 us -> none  [local(): jnp.transpose(local_grad, (1, 0, 2, 3, 4))]
    broadcast_in_dim x4 -> x0, local copies, waits for them, and re-layouts: 110 us -> none  [the longest x1 71.1 us: local(): padded[:, None]]
    conv_general_dilated x2 -> x0, matrix products: 101 us -> none  [correlate(): lax.conv_general_dilated(padded[None], kernel, (1, 1, 1), 'VALID', dimens...]
    broadcast_in_dim x3 -> x0, other arithmetic: 92.5 us -> none  [the longest x2 50.1 us: correlate(): padded[None]]
    conv_general_dilated x8 -> x0, local copies, waits for them, and re-layouts: 90.6 us -> none  [correlate(): lax.conv_general_dilated(padded[None], kernel, (1, 1, 1), 'VALID', dimens...]
    all_to_all x2, blocking collectives: 98.5 us -> 19 us  [to_slabs(): lax.all_to_all(columns, 'gz', split_axis=1, concat_axis=2, tiled=True)]
    reduce_scatter x2 -> x1, waiting for transfers between devices: 55.9 us -> 0.02 us  [local(): lax.psum_scatter(back_terms.astype(bf16), 'col', scatter_dimension=0, til...]
    psum x1, waiting for transfers between devices: 0.03 us -> 55.2 us  [local(): lax.psum(local_grad.reshape(27 * share, channels), 'gz') * scaling]
  transfers between devices with their start and end apart: 9 -> 10, of which waited for: 2 -> 4; matrix products, arithmetic and copies ran while one was open for 55% -> 26% of each run, Pallas kernels for 0% -> 4%
where the time goes in v1:
time: 274 us; the launch traced here: 272 us
  waiting for transfers between devices  71.2 us (26%)
  local copies, waits for them, and re-layouts  55.7 us (20%)
  Pallas kernels  50.7 us (19%)
  other arithmetic  28.1 us (10%)
  blocking collectives  26.1 us (10%)
  starting transfers between devices  22.4 us (8%)
  between operations  16.1 us (6%)
    psum x1, waiting for transfers between devices, local(): lax.psum(local_grad.reshape(27 * share, channels), 'gz') * scaling  55.2 us
    pallas_call x1, Pallas kernels, backward_convs(): pl.pallas_call(partial(back_kernel, rows, size_y), grid=(size_x // rows,)...  25 us
    all_to_all x2, blocking collectives, to_slabs(): lax.all_to_all(columns, 'gz', split_axis=1, concat_axis=2, tiled=True)  19 us
    unnamed x52, local copies, waits for them, and re-layouts  16 us
    pallas_call x1, Pallas kernels, forward_conv(): pl.pallas_call(partial(conv_kernel, rows, size_y), grid=(size_x // rows,)...  11.6 us
    all_to_all x2, starting transfers between devices, to_modes(): lax.all_to_all(planes, 'gz', split_axis=2, concat_axis=1, tiled=True)  11 us
    add x3, local copies, waits for them, and re-layouts, local(): sum((products[:, :, :, z - a + 2, :, z] for z in range(planes)))  9.69 us
    add x1, other arithmetic, local(): sum((products[:, :, :, z - a + 2, :, z] for z in range(planes)))  9.07 us
  transfers between devices with their start and end apart: 10, of which 4 were waited for; matrix products, arithmetic and copies ran while one was open for 26% of the time, Pallas kernels for 4%

profile of v1, /device:TPU:0, one launch (start us, length us, event | category | flops | bytes accessed | tf_op | source)
XLA Modules:
  0.0 272.3 jit_solution(7621127868925133788)
XLA Ops:
  12.8 7.3 %all-to-all-start = ((f32[8,1,1024]{2,1,0:T(1,128)}), f32[8,1,1024]{2,1,0:T(1,128)S(1)}, u32[]{:S(2)}, u32[]{:S(2)}) async-start(f32[8,1,1024]{2,1,0:T(1,128)} %reshape.162), calls=%async_computation | async-start | bytes 65536 | tf_op jit(solution)/shard_map/all_to_all | solution.py:283
  20.1 5.8 %copy.123 = bf16[16,8,128,128]{3,1,2,0:T(8,128)(2,1)S(1)} copy(bf16[16,8,128,128]{3,2,1,0:T(8,128)(2,1)} %bitcast.110) | data formatting | bytes 8388608
  29.9 3.7 %pad_maximum_fusion.f_ref = bf16[128,16640]{1,0:T(8,128)(2,1)} fusion(bf16[128,128]{1,0:T(8,128)(2,1)S(1)} %get-tuple-element.18, bf16[128,16384]{1,0:T(8,128)(2,1)} %bitcast.105, bf16[128,128]{1,0:T(8,128)(2,1)S(1)} %get-tuple-element.17), kind=kLoop, calls=%fused_computation.5 | loop fusion | flops 12779520 | bytes 8519680 | tf_op jit(solution)/shard_map/concatenate | solution.py:302
  33.6 11.6 %forward_conv.1 = f32[64,128,128]{2,1,0:T(8,128)S(1)} custom-call(bf16[128,16640]{1,0:T(8,128)(2,1)} %pad_maximum_fusion.f_ref, bf16[192,384]{1,0:T(8,128)(2,1)S(1)} %copy.89.w_ref), custom_call_target="tpu_custom_call" | custom-call | tf_op jit(solution)/shard_map/forward_conv/pallas_call | solution.py:114
  54.4 7.2 %all_gather.3 = f32[64,16,32]{2,1,0:T(8,128)S(1)} all-gather(f32[16,16,32]{2,1,0:T(8,128)S(1)} %convolution_bitcast_fusion.2), channel_id=1, replica_groups=mesh['gz'=8,'col'=4] {'col'}, dimensions={0}, use_global_device_ids=true | all-gather | bytes 163840 | tf_op jit(solution)/shard_map/all_gather | solution.py:341
  65.1 9.8 %all_to_all.66 = f32[8,1,1024]{2,1,0:T(1,128)S(1)} all-to-all(f32[8,1,1024]{2,1,0:T(1,128)S(1)} %reshape.164), channel_id=1, replica_groups=mesh['gz'=8,'col'=4] {'gz'}, dimensions={0} | all-to-all | bytes 65536 | tf_op jit(solution)/shard_map/all_to_all | solution.py:289
  76.0 8.0 %gelu_stage.1 = (bf16[16,2,128,128]{3,2,1,0:T(8,128)(2,1)}, bf16[16,2,128,128]{3,2,1,0:T(8,128)(2,1)S(1)}, f32[2,16,16,16]{3,2,1,0:T(8,128)S(1)}) custom-call(f32[4,16,128,128]{3,2,1,0:T(8,128)} %bitcast.98, bf16[16,128,128]{2,1,0:T(8,128)(2,1)S(1)} %collective-permute-done.lo_ref, bf16[16,128,128]{2,1,0:T(8,128)(2,1)S(1)} %collective-permute-done.1.hi_ref, ...), custom_call_target="tpu_custom_call" | custom-call | tf_op jit(solution)/shard_map/gelu_stage/pallas_call | solution.py:164
  85.2 4.2 %collective-permute-start.3 = (bf16[16,1,128,128]{3,2,1,0:T(8,128)(2,1)S(1)}, bf16[16,1,128,128]{3,2,1,0:T(8,128)(2,1)}, u32[]{:S(2)}, u32[]{:S(2)}) collective-permute-start(bf16[16,1,128,128]{3,2,1,0:T(8,128)(2,1)S(1)} %get-tuple-element.26), channel_id=1, source_target_pairs={{4,0},{8,4},{12,8},{16,12},{20,16},{24,20},{28,24},{0,28},{5,1},{9... | collective-permute-start | bytes 1572872 | tf_op jit(solution)/shard_map/ppermute | solution.py:356
  89.5 5.1 %copy.95 = bf16[64,2,3,3,16,4]{5,4,3,2,1,0:T(8,128)(2,1)} copy(bf16[64,2,3,3,16,4]{0,5,3,2,4,1:T(4,128)(2,1)} %bitcast.114) | data formatting | bytes 294912 | tf_op jit(solution)/shard_map/transpose;oiabc,azp->oizpbc/transpose | solution.py:333
  94.6 5.8 %reshape.140.w_ref = bf16[128,576]{1,0:T(8,128)(2,1)S(1)} reshape(bf16[64,2,3,3,16,4]{5,4,3,2,1,0:T(8,128)(2,1)} %copy.95) | data formatting | bytes 294912 | tf_op jit(solution)/shard_map/reshape | solution.py:333
  100.4 6.6 %collective-permute-done.2 = bf16[16,1,128,128]{3,2,1,0:T(8,128)(2,1)S(1)} collective-permute-done((bf16[16,1,128,128]{3,2,1,0:T(8,128)(2,1)S(1)}, bf16[16,1,128,128]{3,2,1,0:T(8,128)(2,1)S(1)}, u32[]{:S(2)}, u32[]{:S(2)}) %collective-permute-start.2) | collective-permute-done | bytes 524320 | tf_op jit(solution)/shard_map/ppermute | solution.py:355
  112.6 25.0 %backward_convs.1 = (bf16[128,16384]{1,0:T(8,128)(2,1)}, f32[576,128]{1,0:T(8,128)S(1)}) custom-call(bf16[64,16640]{1,0:T(8,128)(2,1)S(1)} %pad_maximum_fusion.1.g_ref, bf16[128,16384]{1,0:T(8,128)(2,1)} %bitcast.106, bf16[128,576]{1,0:T(8,128)(2,1)S(1)} %reshape.140.w_ref), custom_call_target="tpu_custom_call" | custom-call | tf_op jit(solution)/shard_map/backward_convs/pallas_call | solution.py:230
  137.6 3.2 %dynamic-slice_bitcast_fusion = bf16[2,32,16384]{2,1,0:T(8,128)(2,1)} fusion(bf16[2,2,32,16384]{3,2,1,0:T(8,128)(2,1)} %bitcast.111, s32[]{:T(128)S(6)} %select_n.36), kind=kLoop, calls=%fused_computation.15 | loop fusion | bytes 4194308 | tf_op jit(solution)/shard_map/jit(dynamic_index_in_dim)/squeeze | solution.py:297
  141.9 3.7 %all-to-all-start.2 = ((f32[8,1,1024]{2,1,0:T(1,128)}), f32[8,1,1024]{2,1,0:T(1,128)S(1)}, u32[]{:S(2)}, u32[]{:S(2)}) async-start(f32[8,1,1024]{2,1,0:T(1,128)} %reshape.166), calls=%async_computation.2 | async-start | bytes 65536 | tf_op jit(solution)/shard_map/all_to_all | solution.py:283
  145.8 6.6 %all-to-all-done.2 = f32[8,1,1024]{2,1,0:T(1,128)S(1)} async-done(((f32[8,1,1024]{2,1,0:T(1,128)}), f32[8,1,1024]{2,1,0:T(1,128)S(1)}, u32[]{:S(2)}, u32[]{:S(2)}) %all-to-all-start.2) | async-done | bytes 32800 | tf_op jit(solution)/shard_map/all_to_all | solution.py:283
  158.1 6.7 %reshape.146 = f32[3,3,16,4,64,2]{3,2,1,0,5,4:T(8,128)} reshape(f32[576,128]{0,1:T(8,128)S(1)} %copy.102) | data formatting | bytes 589824 | tf_op jit(solution)/shard_map/reshape | solution.py:377
  164.8 2.8 %fusion.2 = bf16[2,32,16384]{2,1,0:T(8,128)(2,1)S(1)} fusion(bf16[2,32,16384]{2,1,0:T(8,128)(2,1)} %collective-permute-done.4, bf16[2,2,32,16384]{3,2,1,0:T(8,128)(2,1)} %bitcast.112, s32[]{:T(128)S(6)} %select_n.35), kind=kLoop, calls=%fused_computation.10 | loop fusion | flops 4194304 | bytes 6291460 | tf_op jit(solution)/shard_map/convert_element_type | solution.py:370
  169.7 9.1 %slice_add_fusion.2 = (f32[3,3,16,1,64,1]{3,2,1,0,5,4:T(8,128)}, f32[3,3,16,1,64,1]{3,2,1,0,5,4:T(8,128)}, f32[3,3,16,1,64,1]{3,2,1,0,5,4:T(8,128)}) fusion(f32[3,3,16,4,64,2]{3,2,1,0,5,4:T(8,128)S(1)} %copy-done.10), kind=kLoop, calls=%fused_computation.4 | loop fusion | flops 27648 | bytes 331776 | tf_op jit(solution)/shard_map/add | solution.py:379
  178.8 3.2 %copy.103 = f32[3,3,16,1,64,1]{4,2,1,0,5,3:T(8,128)S(1)} copy(f32[3,3,16,1,64,1]{3,2,1,0,5,4:T(8,128)} %get-tuple-element.14) | data formatting | bytes 73728 | tf_op jit(solution)/shard_map/add | solution.py:379
  182.0 3.2 %copy.104 = f32[3,3,16,1,64,1]{4,2,1,0,5,3:T(8,128)S(1)} copy(f32[3,3,16,1,64,1]{3,2,1,0,5,4:T(8,128)} %get-tuple-element.16) | data formatting | bytes 73728 | tf_op jit(solution)/shard_map/add | solution.py:379
  185.2 3.2 %copy.105 = f32[3,3,16,1,64,1]{4,2,1,0,5,3:T(8,128)S(1)} copy(f32[3,3,16,1,64,1]{3,2,1,0,5,4:T(8,128)} %get-tuple-element.15) | data formatting | bytes 73728 | tf_op jit(solution)/shard_map/add | solution.py:379
  190.4 9.2 %all_to_all.67 = f32[8,1,1024]{2,1,0:T(1,128)S(1)} all-to-all(f32[8,1,1024]{2,1,0:T(1,128)S(1)} %reshape.168), channel_id=1, replica_groups=mesh['gz'=8,'col'=4] {'gz'}, dimensions={0} | all-to-all | bytes 65536 | tf_op jit(solution)/shard_map/all_to_all | solution.py:289
  202.2 55.2 %all-reduce.2.cloned.1.call-done = f32[432,64]{1,0:T(8,128)} async-done(((f32[432,64]{1,0:T(8,128)}), f32[432,64]{1,0:T(8,128)}) %all-reduce.2.cloned.1.call-update) | async-done | bytes 110608 | tf_op jit(solution)/shard_map/psum | solution.py:383
  259.5 5.3 %final_stage.1 = bf16[32,128,128]{2,1,0:T(8,128)(2,1)} custom-call(bf16[32,128,128]{2,1,0:T(8,128)(2,1)S(1)} %bitcast.100, bf16[32,128,128]{2,1,0:T(8,128)(2,1)S(1)} %bitcast.101, f32[32,16,16]{2,1,0:T(8,128)S(1)} %reshape.144.s_ref, f32[128,16]{1,0:T(8,128)S(1)} %copy-done.2, f32[16,128]{1,0:T(8,128)S(1)} %copy-done.7), custom_call_target="tpu_custom_call" | custom-call | tf_op jit(solution)/shard_map/final_stage/pallas_call | solution.py:265
  (110 shorter events, 44.5 us)
Async XLA Ops:
  12.8 39.4 %all-to-all-start = ((f32[8,1,1024]{2,1,0:T(1,128)}), f32[8,1,1024]{2,1,0:T(1,128)S(1)}, u32[]{:S(2)}, u32[]{:S(2)}) async-start(f32[8,1,1024]{2,1,0:T(1,128)} %reshape.162), calls=%async_computation | async-start | bytes 65536 | tf_op jit(solution)/shard_map/all_to_all | solution.py:283
  20.1 7.8 %copy-start.16 = (bf16[16,64,27]{1,0,2:T(8,128)(2,1)S(1)}, bf16[16,64,27]{1,0,2:T(8,128)(2,1)}, u32[]{:S(2)}) copy-start(bf16[16,64,27]{1,0,2:T(8,128)(2,1)} %param.12) | copy-start | bytes 165892
  20.1 7.8 %copy-start.19 = (bf16[3,2,4,1,1,1]{0,2,5,4,3,1:T(4,128)(2,1)S(1)}, bf16[3,2,4,1,1,1]{0,2,5,4,3,1:T(4,128)(2,1)}, u32[]{:S(2)}) copy-start(bf16[3,2,4,1,1,1]{0,2,5,4,3,1:T(4,128)(2,1)} %constant.88) | copy-start | bytes 148
  28.2 5.4 %copy-start.13 = (bf16[2,4,16,64,3,3]{3,1,5,4,2,0:T(4,128)(2,1)}, bf16[2,4,16,64,3,3]{3,1,5,4,2,0:T(4,128)(2,1)S(1)}, u32[]{:S(2)}) copy-start(bf16[2,4,16,64,3,3]{3,1,5,4,2,0:T(4,128)(2,1)S(1)} %fusion.3) | copy-start | bytes 442372
  45.2 8.9 %copy-start.18 = (f32[16,16,1]{1,0,2:T(8,128)S(1)}, f32[16,16,1]{1,0,2:T(8,128)}, u32[]{:S(2)}) copy-start(f32[16,16,1]{1,0,2:T(8,128)} %constant.89) | copy-start | bytes 3076
  45.6 19.0 %copy-start.17 = (f32[16,16,1]{0,1,2:T(8,128)S(1)}, f32[16,16,1]{0,1,2:T(8,128)}, u32[]{:S(2)}) copy-start(f32[16,16,1]{0,1,2:T(8,128)} %constant.90) | copy-start | bytes 3076
  45.6 30.3 %copy-start.1 = (bf16[16,2,128,128]{3,2,1,0:T(8,128)(2,1)S(1)}, bf16[16,2,128,128]{3,2,1,0:T(8,128)(2,1)}, u32[]{:S(2)}) copy-start(bf16[16,2,128,128]{3,2,1,0:T(8,128)(2,1)} %g_ref.1) | copy-start | bytes 3145732
  45.7 30.3 %copy-start.2 = (f32[128,16]{1,0:T(8,128)S(1)}, f32[128,16]{1,0:T(8,128)}, u32[]{:S(2)}) copy-start(f32[128,16]{1,0:T(8,128)} %constant.77.clone.ext_ref) | copy-start | bytes 24580
  45.7 30.3 %copy-start.6 = (bf16[128,16]{1,0:T(8,128)(2,1)S(1)}, bf16[128,16]{1,0:T(8,128)(2,1)}, u32[]{:S(2)}) copy-start(bf16[128,16]{1,0:T(8,128)(2,1)} %constant.80.clone.ey_ref.eyt_ref) | copy-start | bytes 12292
  45.7 30.3 %copy-start.7 = (f32[16,128]{1,0:T(8,128)S(1)}, f32[16,128]{1,0:T(8,128)}, u32[]{:S(2)}) copy-start(f32[16,128]{1,0:T(8,128)} %constant.78.clone.ey_ref) | copy-start | bytes 24580
  45.7 30.3 %copy-start.9 = (bf16[32,128]{1,0:T(8,128)(2,1)S(1)}, bf16[32,128]{1,0:T(8,128)(2,1)}, u32[]{:S(2)}) copy-start(bf16[32,128]{1,0:T(8,128)(2,1)} %constant.79.clone.ex_ref.ex2_ref) | copy-start | bytes 24580
  47.5 28.4 %collective-permute-start = (bf16[16,128,128]{2,1,0:T(8,128)(2,1)}, bf16[16,128,128]{2,1,0:T(8,128)(2,1)S(1)}, u32[]{:S(2)}, u32[]{:S(2)}) collective-permute-start(bf16[16,128,128]{2,1,0:T(8,128)(2,1)} %get-tuple-element.24), channel_id=1, source_target_pairs={{0,4},{4,8},{8,12},{12,16},{16,20},{20,24},{24,28},{28,0},{1,5},{5... | collective-permute-start | bytes 1572872 | tf_op jit(solution)/shard_map/ppermute | solution.py:346
  49.5 26.4 %collective-permute-start.1 = (bf16[16,128,128]{2,1,0:T(8,128)(2,1)}, bf16[16,128,128]{2,1,0:T(8,128)(2,1)S(1)}, u32[]{:S(2)}, u32[]{:S(2)}) collective-permute-start(bf16[16,128,128]{2,1,0:T(8,128)(2,1)} %get-tuple-element.23), channel_id=1, source_target_pairs={{4,0},{8,4},{12,8},{16,12},{20,16},{24,20},{28,24},{0,28},{5,1},{9... | collective-permute-start | bytes 1572872 | tf_op jit(solution)/shard_map/ppermute | solution.py:347
  61.8 14.1 %copy-start.14 = (f32[64,16,32]{0,2,1:T(8,128)}, f32[64,16,32]{0,2,1:T(8,128)S(1)}, u32[]{:S(2)}) copy-start(f32[64,16,32]{0,2,1:T(8,128)S(1)} %copy.92) | copy-start | bytes 393220
  84.7 22.3 %collective-permute-start.2 = (bf16[16,1,128,128]{3,2,1,0:T(8,128)(2,1)S(1)}, bf16[16,1,128,128]{3,2,1,0:T(8,128)(2,1)S(1)}, u32[]{:S(2)}, u32[]{:S(2)}) collective-permute-start(bf16[16,1,128,128]{3,2,1,0:T(8,128)(2,1)S(1)} %get-tuple-element.25), channel_id=1, source_target_pairs={{0,4},{4,8},{8,12},{12,16},{16,20},{20,24},{24,28},{28,0},{1,5},{5... | collective-permute-start | bytes 1572872 | tf_op jit(solution)/shard_map/ppermute | solution.py:355
  85.2 24.5 %collective-permute-start.3 = (bf16[16,1,128,128]{3,2,1,0:T(8,128)(2,1)S(1)}, bf16[16,1,128,128]{3,2,1,0:T(8,128)(2,1)}, u32[]{:S(2)}, u32[]{:S(2)}) collective-permute-start(bf16[16,1,128,128]{3,2,1,0:T(8,128)(2,1)S(1)} %get-tuple-element.26), channel_id=1, source_target_pairs={{4,0},{8,4},{12,8},{16,12},{20,16},{24,20},{28,24},{0,28},{5,1},{9... | collective-permute-start | bytes 1572872 | tf_op jit(solution)/shard_map/ppermute | solution.py:356
  112.5 28.2 %copy-start.4 = (f32[2,16,16,16]{3,2,1,0:T(8,128)S(1)}, f32[2,16,16,16]{3,2,1,0:T(8,128)}, u32[]{:S(2)}) copy-start(f32[2,16,16,16]{3,2,1,0:T(8,128)} %copy-done.3) | copy-start | bytes 98308
  137.6 16.4 %copy-start.12 = (bf16[64,16,16,32]{0,3,2,1:T(8,128)(2,1)S(1)}, bf16[64,16,16,32]{0,3,2,1:T(8,128)(2,1)}, u32[]{:S(2)}) copy-start(bf16[64,16,16,32]{0,3,2,1:T(8,128)(2,1)} %param.13) | copy-start | bytes 3145732
  137.6 16.4 %copy-start.15 = (f32[64,16,32]{0,2,1:T(8,128)S(1)}, f32[64,16,32]{0,2,1:T(8,128)}, u32[]{:S(2)}) copy-start(f32[64,16,32]{0,2,1:T(8,128)} %copy-done.14) | copy-start | bytes 393220
  140.8 24.0 %collective-permute-start.4 = (bf16[2,32,16384]{2,1,0:T(8,128)(2,1)}, bf16[2,32,16384]{2,1,0:T(8,128)(2,1)}, u32[]{:S(2)}, u32[]{:S(2)}) collective-permute-start(bf16[2,32,16384]{2,1,0:T(8,128)(2,1)} %dynamic-slice_bitcast_fusion), channel_id=1, source_target_pairs={{0,1},{1,0},{2,3},{3,2},{4,5},{5,4},{6,7},{7,6},{8,9},{9,8},{10,11... | collective-permute-start | bytes 6291464 | tf_op jit(solution)/shard_map/ppermute | solution.py:298
  141.9 10.4 %all-to-all-start.2 = ((f32[8,1,1024]{2,1,0:T(1,128)}), f32[8,1,1024]{2,1,0:T(1,128)S(1)}, u32[]{:S(2)}, u32[]{:S(2)}) async-start(f32[8,1,1024]{2,1,0:T(1,128)} %reshape.166), calls=%async_computation.2 | async-start | bytes 65536 | tf_op jit(solution)/shard_map/all_to_all | solution.py:283
  145.7 43.6 %reduce-scatter.2.cloned.1.call-start = ((), (), s32[]{:S(2)}) async-start(), calls=%async_computation.5 | async-start | bytes 327680 | tf_op jit(solution)/shard_map/reduce_scatter | solution.py:387
  157.6 99.8 %all-reduce.2.cloned.1.call-start = ((), (), s32[]{:S(2)}) async-start(), calls=%async_computation.6 | async-start | bytes 442368 | tf_op jit(solution)/shard_map/psum | solution.py:383
  167.8 91.5 %collective-permute-start.5 = (bf16[1,32,16384]{2,1,0:T(8,128)(2,1)S(1)}, bf16[1,32,16384]{2,1,0:T(8,128)(2,1)S(1)}, u32[]{:S(2)}, u32[]{:S(2)}) collective-permute-start(bf16[1,32,16384]{2,1,0:T(8,128)(2,1)S(1)} %get-tuple-element.19), channel_id=1, source_target_pairs={{0,2},{1,3},{2,0},{3,1},{4,6},{5,7},{6,4},{7,5},{8,10},{9,11},{10,... | collective-permute-start | bytes 3145736 | tf_op jit(solution)/shard_map/ppermute | solution.py:298
  (6 other events, 11.4 us)
Sparse Core Ops, SparseCore 0:
  157.7 18.9 reduce-scatter.1
Sparse Core Ops, SparseCore 1:
  189.3 68.0 all-reduce.1

commit v2 on v1

v2 whole, which is shorter than its diff:
```python
from functools import partial
import math

import jax
import jax.numpy as jnp
import numpy as np
from jax import lax
from jax.experimental import pallas as pl
from jax.experimental.pallas import tpu as pltpu
from jax.sharding import PartitionSpec as P

highest = lax.Precision.HIGHEST
f32 = jnp.float32
bf16 = jnp.bfloat16


def basis(length, mode_count):
    indices = np.arange(mode_count)
    middle = mode_count // 2
    cosine_rows = indices <= middle
    frequency = np.where(cosine_rows, indices, indices - middle)
    residue = frequency[:, None] * np.arange(length)[None, :] % length
    radians = residue * (2.0 * math.pi / length)
    tables = np.where(cosine_rows[:, None], np.cos(radians), np.sin(radians))
    return (tables * math.sqrt(2.0 / length)).astype(np.float32)


def split_table(table):
    high = table.astype(bf16)
    return high, (table - high.astype(np.float32)).astype(bf16)


def neighbours(axis):
    count = lax.axis_size(axis)
    up = [(i, (i + 1) % count) for i in range(count)]
    down = [((i + 1) % count, i) for i in range(count)]
    return up, down


def params(*semantics):
    return pltpu.CompilerParams(
        dimension_semantics=semantics, vmem_limit_bytes=48 * 1024 * 1024
    )


def slab_modes(slab_of, count, ex2, eyt):
    modes = ex2.shape[0] // 2
    parts = []
    for s in range(count):
        both = jnp.dot(ex2, slab_of(s), preferred_element_type=f32)
        parts.append(both[:modes] + both[modes:])
    along_x = jnp.concatenate(parts, axis=0)
    high = along_x.astype(bf16)
    low = (along_x - high.astype(f32)).astype(bf16)
    return jnp.dot(high, eyt, preferred_element_type=f32) + jnp.dot(
        low, eyt, preferred_element_type=f32
    )


def analyse_kernel(v_ref, ex_ref, ey_ref, o_ref):
    count = v_ref.shape[0]
    ex2, eyt = ex_ref[...], ey_ref[...]
    out = slab_modes(lambda s: v_ref[s], count, ex2, eyt)
    o_ref[...] = out.reshape(o_ref.shape)


def analyse_slabs(volume, ex2, eyt):
    slabs, size_x, size_y = volume.shape
    modes = eyt.shape[1]
    block = 16
    return pl.pallas_call(
        analyse_kernel,
        grid=(slabs // block,),
        in_specs=[
            pl.BlockSpec((block, size_x, size_y), lambda g: (g, 0, 0)),
            pl.BlockSpec(ex2.shape, lambda g: (0, 0)),
            pl.BlockSpec(eyt.shape, lambda g: (0, 0)),
        ],
        out_specs=pl.BlockSpec((block, modes, modes), lambda g: (g, 0, 0)),
        out_shape=jax.ShapeDtypeStruct((slabs, modes, modes), f32),
        compiler_params=params("arbitrary"),
        name="analyse",
    )(volume, ex2, eyt)


def chunk_specs(height, rows, size_x, size_y):
    return [
        pl.BlockSpec((height, size_y), lambda g: (0, (g * rows + size_x - 1) % size_x)),
        pl.BlockSpec((height, rows * size_y), lambda g: (0, g)),
        pl.BlockSpec((height, size_y), lambda g: (0, (g * rows + rows) % size_x)),
    ]


def conv_kernel(rows, size_y, low_ref, mid_ref, high_ref, w_ref, o_ref):
    span = rows * size_y
    block = jnp.concatenate([low_ref[...], mid_ref[...], high_ref[...]], axis=1)
    stacked = jnp.concatenate(
        [block[:, b * size_y : b * size_y + span] for b in range(3)], axis=0
    )
    total = jnp.dot(w_ref[...], stacked, preferred_element_type=f32)
    count = total.shape[0] // 3
    flat = o_ref.reshape(count * rows, size_y)
    for r in range(rows):
        piece = total[:, r * size_y : (r + 1) * size_y]
        value = (
            pltpu.roll(piece[:count], 1, 1)
            + piece[count : 2 * count]
            + pltpu.roll(piece[2 * count :], size_y - 1, 1)
        )
        flat[pl.ds(r, count, stride=rows), :] = value


def forward_conv(flat, weights, size_x, size_y):
    count = weights.shape[0] // 3
    rows = 8
    return pl.pallas_call(
        partial(conv_kernel, rows, size_y),
        grid=(size_x // rows,),
        in_specs=chunk_specs(flat.shape[0], rows, size_x, size_y)
        + [pl.BlockSpec(weights.shape, lambda g: (0, 0))],
        out_specs=pl.BlockSpec((count, rows, size_y), lambda g: (0, g, 0)),
        out_shape=jax.ShapeDtypeStruct((count, size_x, size_y), f32),
        compiler_params=params("arbitrary"),
        name="forward_conv",
    )(flat, flat, flat, weights)


def planar(spectrum, ext, ey):
    along_x = jnp.dot(ext, spectrum, precision=highest, preferred_element_type=f32)
    return jnp.dot(along_x, ey, precision=highest, preferred_element_type=f32)


def gelu_kernel(c_ref, lo_ref, hi_ref, s_ref, g_ref, ext_ref, ey_ref, ex2_ref, eyt_ref,
                out_ref, gp_ref, m_ref):
    plane = pl.program_id(0)
    last = pl.num_programs(0) - 1
    count = c_ref.shape[1]
    keep_lo = jnp.where(plane == 0, 1.0, 0.0).astype(f32)
    keep_hi = jnp.where(plane == last, 1.0, 0.0).astype(f32)
    ext, ey = ext_ref[...], ey_ref[...]
    k0 = math.sqrt(2.0 / math.pi)
    k1 = 0.044715
    for o in range(count):
        v = c_ref[0, o] + lo_ref[o].astype(f32) * keep_lo + hi_ref[o].astype(f32) * keep_hi
        v = v + planar(s_ref[0, o], ext, ey)
        v2 = v * v
        t = jnp.tanh(k0 * v * (1.0 + k1 * v2))
        half = 0.5 * (1.0 + t)
        out_ref[o, 0] = (v * half).astype(bf16)
        slope = half + (0.5 * k0) * v * (1.0 - t * t) * (1.0 + (3.0 * k1) * v2)
        gp_ref[0, o] = (g_ref[o, 0].astype(f32) * slope).astype(bf16)
    modes = slab_modes(lambda o: gp_ref[0, o], count, ex2_ref[...], eyt_ref[...])
    m_ref[...] = modes.reshape(m_ref.shape)


def gelu_stage(conv, low, high, slabs, grad_out, tables):
    ext, ey, ex2, eyt = tables
    share, planes, size_x, size_y = grad_out.shape
    modes = ey.shape[0]
    block = 8
    field = pl.BlockSpec((block, 1, size_x, size_y), lambda z, g: (g, z, 0, 0))
    rim = pl.BlockSpec((block, size_x, size_y), lambda z, g: (g, 0, 0))
    whole = lambda t: pl.BlockSpec(t.shape, lambda z, g: (0, 0))
    return pl.pallas_call(
        gelu_kernel,
        grid=(planes, share // block),
        in_specs=[
            pl.BlockSpec((1, block, size_x, size_y), lambda z, g: (z + 1, g, 0, 0)),
            rim,
            rim,
            pl.BlockSpec((1, block, modes, modes), lambda z, g: (z, g, 0, 0)),
            field,
            whole(ext),
            whole(ey),
            whole(ex2),
            whole(eyt),
        ],
        out_specs=[
            field,
            pl.BlockSpec((1, block, size_x, size_y), lambda z, g: (z, g, 0, 0)),
            pl.BlockSpec((1, block, modes, modes), lambda z, g: (z, g, 0, 0)),
        ],
        out_shape=[
            jax.ShapeDtypeStruct(grad_out.shape, bf16),
            jax.ShapeDtypeStruct((planes, share, size_x, size_y), bf16),
            jax.ShapeDtypeStruct((planes, share, modes, modes), f32),
        ],
        compiler_params=params("arbitrary", "arbitrary"),
        name="gelu_stage",
    )(conv, low, high, slabs, grad_out, ext, ey, ex2, eyt)


def back_kernel(rows, size_y, planes, low_ref, mid_ref, high_ref, f_ref, w_ref, c_ref, t_ref,
                acc_ref):
    step = pl.program_id(0)
    height = mid_ref.shape[0]
    depth = f_ref.shape[0]
    span = rows * size_y
    pieces = [low_ref[...]]
    pieces += [mid_ref[:, r * size_y : (r + 1) * size_y] for r in range(rows)]
    pieces.append(high_ref[...])
    wide = [piece.astype(f32) for piece in pieces]
    columns = [
        [pltpu.roll(piece, size_y - 1, 1).astype(bf16) for piece in wide],
        pieces,
        [pltpu.roll(piece, 1, 1).astype(bf16) for piece in wide],
    ]
    columns = [jnp.concatenate(column, axis=1) for column in columns]
    stacked = jnp.concatenate(
        [
            column[:, (2 - b) * size_y : (2 - b) * size_y + span]
            for b in range(3)
            for column in columns
        ],
        axis=0,
    )
    c_ref[...] = jnp.dot(w_ref[...], stacked, preferred_element_type=f32).astype(bf16)
    product = lax.dot_general(
        stacked, f_ref[...], (((1,), (1,)), ((), ())), preferred_element_type=f32
    )

    @pl.when(step == 0)
    def _():
        acc_ref[...] = product

    @pl.when(step > 0)
    def _():
        acc_ref[...] += product

    @pl.when(step == pl.num_programs(0) - 1)
    def _():
        share = height // (planes + 2)
        channels = depth // planes
        for a in range(3):
            for k in range(9):
                total = None
                for z in range(planes):
                    first = k * height + (z - a + 2) * share
                    term = acc_ref[first : first + share, :]
                    if z:
                        term = pltpu.roll(term, depth - z * channels, 1)
                    total = term if total is None else total + term
                out = (9 * a + k) * share
                t_ref[out : out + share, :] = total[:, :channels]


def backward_convs(grads, flat, weights, planes, size_x, size_y):
    height = grads.shape[0]
    depth = flat.shape[0]
    rows = 8
    span = rows * size_y
    taps = (27 * height // (planes + 2), depth // planes)
    return pl.pallas_call(
        partial(back_kernel, rows, size_y, planes),
        grid=(size_x // rows,),
        in_specs=chunk_specs(height, rows, size_x, size_y)
        + [
            pl.BlockSpec((depth, span), lambda g: (0, g)),
            pl.BlockSpec(weights.shape, lambda g: (0, 0)),
        ],
        out_specs=[
            pl.BlockSpec((depth, span), lambda g: (0, g)),
            pl.BlockSpec(taps, lambda g: (0, 0)),
        ],
        out_shape=[
            jax.ShapeDtypeStruct((depth, size_x * size_y), bf16),
            jax.ShapeDtypeStruct(taps, f32),
        ],
        scratch_shapes=[pltpu.VMEM((9 * height, depth), f32)],
        compiler_params=params("arbitrary"),
        name="backward_convs",
    )(grads, grads, grads, flat, weights)


def final_kernel(a_ref, b_ref, s_ref, ext_ref, ey_ref, o_ref):
    ext, ey = ext_ref[...], ey_ref[...]
    for i in range(a_ref.shape[1]):
        total = a_ref[0, i].astype(f32) + b_ref[0, i].astype(f32)
        o_ref[i, 0] = (total + planar(s_ref[0, i], ext, ey)).astype(bf16)


def final_stage(own, other, slabs, tables):
    ext, ey = tables[:2]
    planes, share, size_x, size_y = own.shape
    modes = ey.shape[0]
    block = 8
    field = pl.BlockSpec((1, block, size_x, size_y), lambda z, g: (z, g, 0, 0))
    return pl.pallas_call(
        final_kernel,
        grid=(planes, share // block),
        in_specs=[
            field,
            field,
            pl.BlockSpec((1, block, modes, modes), lambda z, g: (z, g, 0, 0)),
            pl.BlockSpec(ext.shape, lambda z, g: (0, 0)),
            pl.BlockSpec(ey.shape, lambda z, g: (0, 0)),
        ],
        out_specs=pl.BlockSpec((block, 1, size_x, size_y), lambda z, g: (g, z, 0, 0)),
        out_shape=jax.ShapeDtypeStruct((share, planes, size_x, size_y), bf16),
        compiler_params=params("arbitrary", "arbitrary"),
        name="final_stage",
    )(own, other, slabs, ext, ey)


def to_modes(planes, table_z):
    gathered = lax.all_to_all(planes, "gz", split_axis=2, concat_axis=1, tiled=True)
    return jnp.einsum("jz,czm->cjm", table_z, gathered, precision=highest)


def to_slabs(spectrum, table_z):
    columns = jnp.einsum("jz,cjm->czm", table_z, spectrum, precision=highest)
    return lax.all_to_all(columns, "gz", split_axis=1, concat_axis=2, tiled=True)


def plane_slabs(spectrum, table_z, planes):
    slabs = to_slabs(spectrum, table_z)
    modes = table_z.shape[0]
    return jnp.transpose(slabs.reshape(-1, planes, modes, modes), (1, 0, 2, 3))


def halve(block, bit):
    count = lax.axis_size("col")
    side = (lax.axis_index("col") // bit) % 2
    pairs = [(i, i ^ bit) for i in range(count)]
    mine = lax.dynamic_index_in_dim(block, side, 2, keepdims=False)
    other = lax.dynamic_index_in_dim(block, 1 - side, 2, keepdims=False)
    return mine, lax.ppermute(other, "col", pairs)


def sum_over_slabs(terms):
    groups = lax.axis_size("gz")
    pieces = lax.all_to_all(terms.reshape(groups, -1), "gz", split_axis=0, concat_axis=0, tiled=True)
    total = lax.all_gather(jnp.sum(pieces, axis=0), "gz", axis=0, tiled=True)
    return total.reshape(terms.shape)


def local(features, grad_out, conv_weight, spectral_weight):
    channels, planes, size_x, size_y = features.shape
    share = conv_weight.shape[0]
    modes = spectral_weight.shape[2]
    groups = lax.axis_size("gz")
    parts = lax.axis_size("col")
    table_x = basis(size_x, modes)
    table_y = basis(size_y, modes)
    table_z = basis(planes * groups, modes)
    ex2 = np.concatenate(split_table(table_x), axis=0)
    eyt = np.ascontiguousarray(table_y.astype(bf16).T)
    tables = tuple(
        jnp.asarray(t) for t in (np.ascontiguousarray(table_x.T), table_y, ex2, eyt)
    )
    table_z = jnp.asarray(table_z)
    up, down = neighbours("gz")

    taps = conv_weight.reshape(share, channels, 3, 9)[:, :, ::-1]
    taps = jnp.transpose(taps, (1, 3, 2, 0)).reshape(channels, 9, 3 * share)
    w_back = jnp.stack(
        [
            jnp.pad(taps, ((0, 0), (0, 0), (z * share, (planes - 1 - z) * share)))
            for z in range(planes)
        ]
    ).reshape(planes * channels, 9 * share * (planes + 2))
    thirds = w_back.shape[1] // 3
    w_forward = jnp.concatenate(
        [w_back[:, b * thirds : (b + 1) * thirds].T for b in range(3)], axis=1
    )

    first_channel = lax.axis_index("col") * share
    own = lax.dynamic_slice_in_dim(features, first_channel, share, 0)
    planar_modes = analyse_slabs(own.reshape(share * planes, size_x, size_y), *tables[2:])
    spectrum = to_modes(planar_modes.reshape(share, planes, modes * modes), table_z)
    spectrum_all = lax.all_gather(spectrum, "col", axis=0, tiled=True)

    flat = jnp.transpose(features, (1, 0, 2, 3)).reshape(planes * channels, size_x * size_y)
    conv = forward_conv(flat, w_forward, size_x, size_y)
    conv = conv.reshape(planes + 2, share, size_x, size_y)
    low = lax.ppermute(conv[planes + 1].astype(bf16), "gz", up)
    high = lax.ppermute(conv[0].astype(bf16), "gz", down)

    weights32 = spectral_weight.astype(f32)
    mixed = jnp.sum(weights32 * spectrum_all[:, None], axis=0)
    slabs = plane_slabs(mixed, table_z, planes)
    layer_out, grad_pre, grad_planar = gelu_stage(conv, low, high, slabs, grad_out, tables)

    before = lax.ppermute(grad_pre[planes - 1 :], "gz", up)
    after = lax.ppermute(grad_pre[:1], "gz", down)
    grad_planar = jnp.transpose(grad_planar, (1, 0, 2, 3)).reshape(share, planes, modes * modes)
    grad_modes = to_modes(grad_planar, table_z)

    rimmed = jnp.concatenate([before, grad_pre, after], axis=0)
    rimmed = rimmed.reshape((planes + 2) * share, size_x * size_y)
    contributions, products = backward_convs(rimmed, flat, w_back, planes, size_x, size_y)
    block = contributions.reshape(planes, parts, share, size_x * size_y)
    bit = 1
    received = None
    while bit < parts:
        if received is not None:
            block = (block.astype(f32) + received.astype(f32)).astype(bf16)
        paired = block.reshape(planes, block.shape[1] // 2, 2, *block.shape[2:])
        block, received = halve(paired, bit)
        bit *= 2
    shape = (planes, share, size_x, size_y)
    block, received = block.reshape(shape), received.reshape(shape)

    scaling = 1.0 / math.sqrt(size_x * size_y * planes * groups)
    grad_conv = sum_over_slabs(products) * scaling
    grad_conv = jnp.transpose(grad_conv.reshape(27, share, channels), (1, 2, 0))

    back_terms = jnp.sum(weights32 * grad_modes[None], axis=1)
    back_modes = lax.psum_scatter(
        back_terms.astype(bf16), "col", scatter_dimension=0, tiled=True
    ).astype(f32)
    back_slabs = plane_slabs(back_modes, table_z, planes)
    grad_input = final_stage(block, received, back_slabs, tables)
    grad_spectral = spectrum_all[:, None] * grad_modes[None]
    return (layer_out, grad_input, grad_conv, grad_spectral)


def solution(mesh):
    return jax.shard_map(
        local,
        mesh=mesh,
        in_specs=(
            P(None, "gz", None, None),
            P("col", "gz", None, None),
            P("col", None, None),
            P(None, "col", None, "gz"),
        ),
        out_specs=(
            P("col", "gz", None, None),
            P("col", "gz", None, None),
            P("col", None, None),
            P(None, "col", None, "gz"),
        ),
        check_vma=False,
    )
```

time: 274 us -> 242 us (0.88)
  local copies, waits for them, and re-layouts: 55.7 us -> 32.3 us
  blocking collectives: 26.1 us -> 47.6 us
  waiting for transfers between devices: 71.2 us -> 55.8 us
  other arithmetic: 28.1 us -> 14.4 us
  starting transfers between devices: 22.4 us -> 31 us
  Pallas kernels: 50.7 us -> 42.9 us
    psum x1 -> x0, waiting for transfers between devices: 55.2 us -> none  [local(): lax.psum(local_grad.reshape(27 * share, channels), 'gz') * scaling]
    all_gather x0 -> x1, blocking collectives: none -> 30.6 us  [sum_over_slabs(): total = lax.all_gather(jnp.sum(pieces, axis=0), 'gz', axis=0, tiled=True)]
    reduce_scatter x1, waiting for transfers between devices: 0.02 us -> 18.4 us  [local(): lax.psum_scatter(back_terms.astype(bf16), 'col', scatter_dimension=0, til...]
    reshape x6 -> x4, local copies, waits for them, and re-layouts: 14.4 us -> 1.42 us  [the longest x2 1.1 us: plane_slabs(): return jnp.transpose(slabs.reshape(-1, planes, modes, modes), (1, 0, 2, 3))]
    ppermute x2, waiting for transfers between devices: 9.33 us -> 20.1 us  [the longest x1 17.4 us: local(): before = lax.ppermute(grad_pre[planes - 1:], 'gz', up)]
    all_to_all x0 -> x2, waiting for transfers between devices: none -> 10.6 us  [the longest x1 5.87 us: to_slabs(): lax.all_to_all(columns, 'gz', split_axis=1, concat_axis=2, tiled=True)]
    add x3 -> x0, local copies, waits for them, and re-layouts: 9.69 us -> none  [local(): sum((products[:, :, :, z - a + 2, :, z] for z in range(planes)))]
    all_to_all x2 -> x1, blocking collectives: 19 us -> 9.82 us  [to_slabs(): lax.all_to_all(columns, 'gz', split_axis=1, concat_axis=2, tiled=True)]
  transfers between devices with their start and end apart: 10 -> 11, of which waited for: 4 -> 6; matrix products, arithmetic and copies ran while one was open for 26% -> 14% of each run, Pallas kernels for 4% -> 5%
where the time goes in v2:
time: 242 us; the launch traced here: 240 us
  waiting for transfers between devices  55.8 us (23%)
  blocking collectives  47.6 us (20%)
  Pallas kernels  42.9 us (18%)
  local copies, waits for them, and re-layouts  32.3 us (13%)
  starting transfers between devices  31 us (13%)
  between operations  14.6 us (6%)
  other arithmetic  14.4 us (6%)
    all_gather x1, blocking collectives, sum_over_slabs(): total = lax.all_gather(jnp.sum(pieces, axis=0), 'gz', axis=0, tiled=True)  30.6 us
    reduce_scatter x1, waiting for transfers between devices, local(): lax.psum_scatter(back_terms.astype(bf16), 'col', scatter_dimension=0, til...  18.4 us
    ppermute x1, waiting for transfers between devices, local(): before = lax.ppermute(grad_pre[planes - 1:], 'gz', up)  17.4 us
    pallas_call x1, Pallas kernels, backward_convs(): pl.pallas_call(partial(back_kernel, rows, size_y, planes), grid=(size_x /...  16.7 us
    unnamed x45, local copies, waits for them, and re-layouts  13.8 us
    pallas_call x1, Pallas kernels, forward_conv(): pl.pallas_call(partial(conv_kernel, rows, size_y), grid=(size_x // rows,)...  12.2 us
    all_to_all x2, starting transfers between devices, to_modes(): lax.all_to_all(planes, 'gz', split_axis=2, concat_axis=1, tiled=True)  11.4 us
    all_to_all x1, blocking collectives, to_slabs(): lax.all_to_all(columns, 'gz', split_axis=1, concat_axis=2, tiled=True)  9.82 us
  transfers between devices with their start and end apart: 11, of which 6 were waited for; matrix products, arithmetic and copies ran while one was open for 14% of the time, Pallas kernels for 5%

profile of v2, /device:TPU:0, one launch (start us, length us, event | category | flops | bytes accessed | tf_op | source)
XLA Modules:
  0.0 240.5 jit_solution(13460622638505573517)
XLA Ops:
  10.6 7.3 %all-to-all-start = ((f32[8,1,1024]{2,1,0:T(1,128)}), f32[8,1,1024]{2,1,0:T(1,128)S(1)}, u32[]{:S(2)}, u32[]{:S(2)}) async-start(f32[8,1,1024]{2,1,0:T(1,128)} %reshape.102), calls=%async_computation | async-start | bytes 65536 | tf_op jit(solution)/shard_map/all_to_all | solution.py:306
  18.6 2.5 %copy.58 = bf16[2,64,128,128]{3,2,1,0:T(8,128)(2,1)S(1)} copy(bf16[2,64,128,128]{3,2,0,1:T(8,128)(2,1)} %bitcast.117) | data formatting | bytes 8388608 | tf_op jit(solution)/shard_map/transpose | solution.py:373
  21.1 5.6 %copy.91 = bf16[16,8,128,128]{3,1,2,0:T(8,128)(2,1)} copy(bf16[16,8,128,128]{3,2,1,0:T(8,128)(2,1)S(1)} %bitcast.115) | data formatting | bytes 8388608
  26.8 12.2 %forward_conv.1 = f32[64,128,128]{2,1,0:T(8,128)S(1)} custom-call(bf16[128,16384]{1,0:T(8,128)(2,1)} %bitcast.111, bf16[128,16384]{1,0:T(8,128)(2,1)} %bitcast.112, bf16[128,16384]{1,0:T(8,128)(2,1)} %bitcast.113, bf16[192,384]{1,0:T(8,128)(2,1)S(1)} %pad_maximum_fusion.2.w_ref), custom_call_target="tpu_custom_call" | custom-call | tf_op jit(solution)/shard_map/forward_conv/pallas_call | solution.py:116
  44.1 2.7 %collective-permute-start.1 = (bf16[16,128,128]{2,1,0:T(8,128)(2,1)}, bf16[16,128,128]{2,1,0:T(8,128)(2,1)S(1)}, u32[]{:S(2)}, u32[]{:S(2)}) collective-permute-start(bf16[16,128,128]{2,1,0:T(8,128)(2,1)} %get-tuple-element.18), channel_id=1, source_target_pairs={{4,0},{8,4},{12,8},{16,12},{20,16},{24,20},{28,24},{0,28},{5,1},{9... | collective-permute-start | bytes 1572872 | tf_op jit(solution)/shard_map/ppermute | solution.py:377
  48.8 7.2 %all_gather.6 = f32[64,16,32]{2,1,0:T(8,128)S(1)} all-gather(f32[16,16,32]{2,1,0:T(8,128)S(1)} %convolution_bitcast_fusion.2), channel_id=1, replica_groups=mesh['gz'=8,'col'=4] {'col'}, dimensions={0}, use_global_device_ids=true | all-gather | bytes 163840 | tf_op jit(solution)/shard_map/all_gather | solution.py:371
  56.3 2.9 %fusion = f32[16,16,32]{2,1,0:T(8,128)S(1)} fusion(bf16[64,16,16,32]{0,3,2,1:T(8,128)(2,1)} %param.12, f32[64,16,32]{0,2,1:T(8,128)S(1)} %copy.63), kind=kLoop, calls=%fused_computation.2 | loop fusion | flops 1564672 | bytes 1212416 | tf_op jit(solution)/shard_map/reduce_sum | solution.py:380
  59.6 9.8 %all_to_all.76 = f32[8,1,1024]{2,1,0:T(1,128)S(1)} all-to-all(f32[8,1,1024]{2,1,0:T(1,128)S(1)} %reshape.104), channel_id=1, replica_groups=mesh['gz'=8,'col'=4] {'gz'}, dimensions={0} | all-to-all | bytes 65536 | tf_op jit(solution)/shard_map/all_to_all | solution.py:312
  70.4 7.9 %gelu_stage.1 = (bf16[16,2,128,128]{3,2,1,0:T(8,128)(2,1)}, bf16[2,16,128,128]{3,2,1,0:T(8,128)(2,1)S(1)}, f32[2,16,16,16]{3,2,1,0:T(8,128)S(1)}) custom-call(f32[4,16,128,128]{3,2,1,0:T(8,128)} %bitcast.101, bf16[16,128,128]{2,1,0:T(8,128)(2,1)S(1)} %collective-permute-done.lo_ref, bf16[16,128,128]{2,1,0:T(8,128)(2,1)S(1)} %collective-permute-done.1.hi_ref, ...), custom_call_target="tpu_custom_call" | custom-call | tf_op jit(solution)/shard_map/gelu_stage/pallas_call | solution.py:164
  79.0 4.2 %collective-permute-start.3 = (bf16[1,16,128,128]{3,2,1,0:T(8,128)(2,1)S(1)}, bf16[1,16,128,128]{3,2,1,0:T(8,128)(2,1)}, u32[]{:S(2)}, u32[]{:S(2)}) collective-permute-start(bf16[1,16,128,128]{3,2,1,0:T(8,128)(2,1)S(1)} %get-tuple-element.21), channel_id=1, source_target_pairs={{4,0},{8,4},{12,8},{16,12},{20,16},{24,20},{28,24},{0,28},{5,1},{9... | collective-permute-start | bytes 1572872 | tf_op jit(solution)/shard_map/ppermute | solution.py:385
  83.4 17.4 %collective-permute-done.2 = bf16[1,16,128,128]{3,2,1,0:T(8,128)(2,1)S(1)} collective-permute-done((bf16[1,16,128,128]{3,2,1,0:T(8,128)(2,1)S(1)}, bf16[1,16,128,128]{3,2,1,0:T(8,128)(2,1)S(1)}, u32[]{:S(2)}, u32[]{:S(2)}) %collective-permute-start.2) | collective-permute-done | bytes 524320 | tf_op jit(solution)/shard_map/ppermute | solution.py:384
  100.7 2.7 %collective-permute-done.3 = bf16[1,16,128,128]{3,2,1,0:T(8,128)(2,1)} collective-permute-done((bf16[1,16,128,128]{3,2,1,0:T(8,128)(2,1)S(1)}, bf16[1,16,128,128]{3,2,1,0:T(8,128)(2,1)}, u32[]{:S(2)}, u32[]{:S(2)}) %collective-permute-start.3) | collective-permute-done | bytes 524320 | tf_op jit(solution)/shard_map/ppermute | solution.py:385
  106.2 16.7 %backward_convs.1 = (bf16[128,16384]{1,0:T(8,128)(2,1)}, f32[432,64]{1,0:T(8,128)S(1)}) custom-call(bf16[64,16384]{1,0:T(8,128)(2,1)S(1)} %bitcast.102, bf16[64,16384]{1,0:T(8,128)(2,1)S(1)} %bitcast.103, bf16[64,16384]{1,0:T(8,128)(2,1)S(1)} %bitcast.104, bf16[128,16384]{1,0:T(8,128)(2,1)} %bitcast.114, bf16[128,576]{1,0:T(8,128)(2,1)S(1)} %copy.66.w_ref), custom_call_target="tpu_custom_call" | custom-call | tf_op jit(solution)/shard_map/backward_convs/pallas_call | solution.py:253
  122.8 2.5 %constant_dynamic-slice_fusion.3 = (bf16[2,2,1,16,16384]{4,3,2,1,0:T(8,128)(2,1)S(1)}, bf16[2,2,1,16,16384]{4,3,2,1,0:T(8,128)(2,1)S(1)}) fusion(bf16[2,2,2,16,16384]{4,3,2,1,0:T(8,128)(2,1)} %bitcast.119, s32[]{:T(128)S(6)} %select_n.35, s32[]{:T(128)S(6)} %select_n.36), kind=kLoop, calls=%fused_computation.30 | loop fusion | bytes 8388616 | tf_op jit(solution)/shard_map/jit(dynamic_index_in_dim)/dynamic_slice | solution.py:325
  128.0 4.2 %all-to-all-start.2 = ((f32[8,1,1024]{2,1,0:T(1,128)}), f32[8,1,1024]{2,1,0:T(1,128)S(1)}, u32[]{:S(2)}, u32[]{:S(2)}) async-start(f32[8,1,1024]{2,1,0:T(1,128)} %reshape.106), calls=%async_computation.2 | async-start | bytes 65536 | tf_op jit(solution)/shard_map/all_to_all | solution.py:306
  132.2 6.6 %all-to-all-done.2 = f32[8,1,1024]{2,1,0:T(1,128)S(1)} async-done(((f32[8,1,1024]{2,1,0:T(1,128)}), f32[8,1,1024]{2,1,0:T(1,128)S(1)}, u32[]{:S(2)}, u32[]{:S(2)}) %all-to-all-start.2) | async-done | bytes 32800 | tf_op jit(solution)/shard_map/all_to_all | solution.py:306
  144.2 3.3 %broadcast_multiply_fusion = (f32[64,16,16,32]{0,3,2,1:T(8,128)}, bf16[64,16,32]{0,2,1:T(8,128)(2,1)}) fusion(f32[16,16,32]{2,1,0:T(8,128)S(1)} %convolution_bitcast_fusion, f32[64,16,32]{0,2,1:T(8,128)S(1)} %copy-done.10, bf16[64,16,16,32]{0,3,2,1:T(8,128)(2,1)S(1)} %copy-done.8), kind=kLoop, calls=%fused_computation.11 | loop fusion | flops 2064384 | bytes 3375104 | tf_op jit(solution)/shard_map/mul | solution.py:414
  149.4 18.4 %reduce-scatter.2.cloned.1.call-done = bf16[16,16,32]{2,1,0:T(8,128)(2,1)} async-done(((bf16[64,16,32]{2,1,0:T(8,128)(2,1)}), bf16[16,16,32]{2,1,0:T(8,128)(2,1)}) %reduce-scatter.2.cloned.1.call-update) | async-done | bytes 16400 | tf_op jit(solution)/shard_map/reduce_scatter | solution.py:409
  171.1 4.5 %all-to-all-start.3 = ((f32[8,1,1024]{2,1,0:T(1,128)}), f32[8,1,1024]{2,1,0:T(1,128)S(1)}, u32[]{:S(2)}, u32[]{:S(2)}) async-start(f32[8,1,1024]{2,1,0:T(1,128)} %reshape.108), calls=%async_computation.4 | async-start | bytes 65536 | tf_op jit(solution)/shard_map/all_to_all | solution.py:312
  176.5 5.9 %all-to-all-done.3 = f32[8,1,1024]{2,1,0:T(1,128)S(1)} async-done(((f32[8,1,1024]{2,1,0:T(1,128)}), f32[8,1,1024]{2,1,0:T(1,128)S(1)}, u32[]{:S(2)}, u32[]{:S(2)}) %all-to-all-start.3) | async-done | bytes 32800 | tf_op jit(solution)/shard_map/all_to_all | solution.py:312
  182.4 4.0 %all-to-all-start.4 = ((f32[8,1,3456]{2,1,0:T(1,128)}), f32[8,1,3456]{2,1,0:T(1,128)}, u32[]{:S(2)}, u32[]{:S(2)}) async-start(f32[8,1,3456]{2,1,0:T(1,128)} %all_to_all.70), calls=%async_computation.5 | async-start | bytes 221184 | tf_op jit(solution)/shard_map/all_to_all | solution.py:332
  188.8 4.8 %all-to-all-done.4 = f32[8,1,3456]{2,1,0:T(1,128)} async-done(((f32[8,1,3456]{2,1,0:T(1,128)}), f32[8,1,3456]{2,1,0:T(1,128)}, u32[]{:S(2)}, u32[]{:S(2)}) %all-to-all-start.4) | async-done | bytes 110624 | tf_op jit(solution)/shard_map/all_to_all | solution.py:332
  194.6 30.6 %all-gather = f32[8,1,3456]{2,1,0:T(1,128)S(1)} all-gather(f32[1,1,3456]{2,1,0:T(1,128)S(1)} %reshape.94), channel_id=1, replica_groups=mesh['gz'=8,'col'=4] {'gz'}, dimensions={0}, use_global_device_ids=true | all-gather | bytes 124416 | tf_op jit(solution)/shard_map/all_gather | solution.py:333
  228.3 5.3 %final_stage.1 = bf16[16,2,128,128]{3,2,1,0:T(8,128)(2,1)} custom-call(bf16[2,16,128,128]{3,2,1,0:T(8,128)(2,1)S(1)} %bitcast.106, bf16[2,16,128,128]{3,2,1,0:T(8,128)(2,1)S(1)} %bitcast.107, f32[2,16,16,16]{3,2,1,0:T(8,128)S(1)} %bitcast.109, f32[128,16]{1,0:T(8,128)S(1)} %copy-done.2, f32[16,128]{1,0:T(8,128)S(1)} %copy-done.6), custom_call_target="tpu_custom_call" | custom-call | tf_op jit(solution)/shard_map/final_stage/pallas_call | solution.py:288
  (101 shorter events, 36.6 us)
Async XLA Ops:
  7.2 10.7 %copy-start.13 = (bf16[16,64,27]{1,0,2:T(8,128)(2,1)S(1)}, bf16[16,64,27]{1,0,2:T(8,128)(2,1)}, u32[]{:S(2)}) copy-start(bf16[16,64,27]{1,0,2:T(8,128)(2,1)} %param.11) | copy-start | bytes 165892
  10.6 36.2 %all-to-all-start = ((f32[8,1,1024]{2,1,0:T(1,128)}), f32[8,1,1024]{2,1,0:T(1,128)S(1)}, u32[]{:S(2)}, u32[]{:S(2)}) async-start(f32[8,1,1024]{2,1,0:T(1,128)} %reshape.102), calls=%async_computation | async-start | bytes 65536 | tf_op jit(solution)/shard_map/all_to_all | solution.py:306
  18.6 2.6 %copy-start.11 = (bf16[128,576]{0,1:T(8,128)(2,1)}, bf16[128,576]{0,1:T(8,128)(2,1)S(1)}, u32[]{:S(2)}) copy-start(bf16[128,576]{0,1:T(8,128)(2,1)S(1)} %reshape.75) | copy-start | bytes 442372
  39.0 2.0 copy-start
  41.0 7.5 %copy-start.15 = (f32[16,16,1]{1,0,2:T(8,128)S(1)}, f32[16,16,1]{1,0,2:T(8,128)}, u32[]{:S(2)}) copy-start(f32[16,16,1]{1,0,2:T(8,128)} %constant.91) | copy-start | bytes 3076
  42.1 28.3 %collective-permute-start = (bf16[16,128,128]{2,1,0:T(8,128)(2,1)}, bf16[16,128,128]{2,1,0:T(8,128)(2,1)S(1)}, u32[]{:S(2)}, u32[]{:S(2)}) collective-permute-start(bf16[16,128,128]{2,1,0:T(8,128)(2,1)} %get-tuple-element.19), channel_id=1, source_target_pairs={{0,4},{4,8},{8,12},{12,16},{16,20},{20,24},{24,28},{28,0},{1,5},{5... | collective-permute-start | bytes 1572872 | tf_op jit(solution)/shard_map/ppermute | solution.py:376
  44.1 26.3 %collective-permute-start.1 = (bf16[16,128,128]{2,1,0:T(8,128)(2,1)}, bf16[16,128,128]{2,1,0:T(8,128)(2,1)S(1)}, u32[]{:S(2)}, u32[]{:S(2)}) collective-permute-start(bf16[16,128,128]{2,1,0:T(8,128)(2,1)} %get-tuple-element.18), channel_id=1, source_target_pairs={{4,0},{8,4},{12,8},{16,12},{20,16},{24,20},{28,24},{0,28},{5,1},{9... | collective-permute-start | bytes 1572872 | tf_op jit(solution)/shard_map/ppermute | solution.py:377
  48.5 10.6 %copy-start.14 = (f32[16,16,1]{0,1,2:T(8,128)S(1)}, f32[16,16,1]{0,1,2:T(8,128)}, u32[]{:S(2)}) copy-start(f32[16,16,1]{0,1,2:T(8,128)} %constant.92) | copy-start | bytes 3076
  56.2 14.1 %copy-start.9 = (f32[64,16,32]{0,2,1:T(8,128)}, f32[64,16,32]{0,2,1:T(8,128)S(1)}, u32[]{:S(2)}) copy-start(f32[64,16,32]{0,2,1:T(8,128)S(1)} %copy.63) | copy-start | bytes 393220
  56.3 14.1 %copy-start.1 = (bf16[16,2,128,128]{3,2,1,0:T(8,128)(2,1)S(1)}, bf16[16,2,128,128]{3,2,1,0:T(8,128)(2,1)}, u32[]{:S(2)}) copy-start(bf16[16,2,128,128]{3,2,1,0:T(8,128)(2,1)} %g_ref.1) | copy-start | bytes 3145732
  56.3 14.1 %copy-start.2 = (f32[128,16]{1,0:T(8,128)S(1)}, f32[128,16]{1,0:T(8,128)}, u32[]{:S(2)}) copy-start(f32[128,16]{1,0:T(8,128)} %constant.77.clone.ext_ref) | copy-start | bytes 24580
  56.3 14.1 %copy-start.6 = (f32[16,128]{1,0:T(8,128)S(1)}, f32[16,128]{1,0:T(8,128)}, u32[]{:S(2)}) copy-start(f32[16,128]{1,0:T(8,128)} %constant.78.clone.ey_ref) | copy-start | bytes 24580
  78.3 4.9 %copy-start.12 = (bf16[128,576]{0,1:T(8,128)(2,1)S(1)}, bf16[128,576]{0,1:T(8,128)(2,1)}, u32[]{:S(2)}) copy-start(bf16[128,576]{0,1:T(8,128)(2,1)} %copy-done.11) | copy-start | bytes 442372
  78.4 22.3 %collective-permute-start.2 = (bf16[1,16,128,128]{3,2,1,0:T(8,128)(2,1)S(1)}, bf16[1,16,128,128]{3,2,1,0:T(8,128)(2,1)S(1)}, u32[]{:S(2)}, u32[]{:S(2)}) collective-permute-start(bf16[1,16,128,128]{3,2,1,0:T(8,128)(2,1)S(1)} %get-tuple-element.20), channel_id=1, source_target_pairs={{0,4},{4,8},{8,12},{12,16},{16,20},{20,24},{24,28},{28,0},{1,5},{5... | collective-permute-start | bytes 1572872 | tf_op jit(solution)/shard_map/ppermute | solution.py:384
  79.0 24.5 %collective-permute-start.3 = (bf16[1,16,128,128]{3,2,1,0:T(8,128)(2,1)S(1)}, bf16[1,16,128,128]{3,2,1,0:T(8,128)(2,1)}, u32[]{:S(2)}, u32[]{:S(2)}) collective-permute-start(bf16[1,16,128,128]{3,2,1,0:T(8,128)(2,1)S(1)} %get-tuple-element.21), channel_id=1, source_target_pairs={{4,0},{8,4},{12,8},{16,12},{20,16},{24,20},{28,24},{0,28},{5,1},{9... | collective-permute-start | bytes 1572872 | tf_op jit(solution)/shard_map/ppermute | solution.py:385
  125.3 1.5 copy-start.4
  126.8 13.5 %collective-permute-start.4 = (bf16[2,2,16,16384]{3,2,0,1:T(8,128)(2,1)}, bf16[2,2,16,16384]{3,2,0,1:T(8,128)(2,1)}, u32[]{:S(2)}, u32[]{:S(2)}) collective-permute-start(bf16[2,2,16,16384]{3,2,0,1:T(8,128)(2,1)} %bitcast.96), channel_id=1, source_target_pairs={{0,1},{1,0},{2,3},{3,2},{4,5},{5,4},{6,7},{7,6},{8,9},{9,8},{10,11... | collective-permute-start | bytes 6291464 | tf_op jit(solution)/shard_map/ppermute | solution.py:327
  128.0 10.9 %all-to-all-start.2 = ((f32[8,1,1024]{2,1,0:T(1,128)}), f32[8,1,1024]{2,1,0:T(1,128)S(1)}, u32[]{:S(2)}, u32[]{:S(2)}) async-start(f32[8,1,1024]{2,1,0:T(1,128)} %reshape.106), calls=%async_computation.2 | async-start | bytes 65536 | tf_op jit(solution)/shard_map/all_to_all | solution.py:306
  132.1 35.7 %reduce-scatter.2.cloned.1.call-start = ((), (), s32[]{:S(2)}) async-start(), calls=%async_computation.6 | async-start | bytes 327680 | tf_op jit(solution)/shard_map/reduce_scatter | solution.py:409
  142.4 1.8 copy-start.8
  142.4 1.8 copy-start.10
  142.6 85.5 %collective-permute-start.5 = (bf16[2,1,16,16384]{3,2,0,1:T(8,128)(2,1)S(1)}, bf16[2,1,16,16384]{3,2,0,1:T(8,128)(2,1)S(1)}, u32[]{:S(2)}, u32[]{:S(2)}) collective-permute-start(bf16[2,1,16,16384]{3,2,0,1:T(8,128)(2,1)S(1)} %get-tuple-element.16), channel_id=1, source_target_pairs={{0,2},{1,3},{2,0},{3,1},{4,6},{5,7},{6,4},{7,5},{8,10},{9,11},{10,... | collective-permute-start | bytes 3145736 | tf_op jit(solution)/shard_map/ppermute | solution.py:327
  171.1 11.2 %all-to-all-start.3 = ((f32[8,1,1024]{2,1,0:T(1,128)}), f32[8,1,1024]{2,1,0:T(1,128)S(1)}, u32[]{:S(2)}, u32[]{:S(2)}) async-start(f32[8,1,1024]{2,1,0:T(1,128)} %reshape.108), calls=%async_computation.4 | async-start | bytes 65536 | tf_op jit(solution)/shard_map/all_to_all | solution.py:312
  182.4 11.2 %all-to-all-start.4 = ((f32[8,1,3456]{2,1,0:T(1,128)}), f32[8,1,3456]{2,1,0:T(1,128)}, u32[]{:S(2)}, u32[]{:S(2)}) async-start(f32[8,1,3456]{2,1,0:T(1,128)} %all_to_all.70), calls=%async_computation.5 | async-start | bytes 221184 | tf_op jit(solution)/shard_map/all_to_all | solution.py:332
  (3 other events, 3.5 us)
Sparse Core Ops, SparseCore 0:
  149.5 18.2 reduce-scatter.1

commit v3 on v2

--- a/solution.py
+++ b/solution.py
@@ -330,7 +330,8 @@
 def sum_over_slabs(terms):
     groups = lax.axis_size("gz")
     pieces = lax.all_to_all(terms.reshape(groups, -1), "gz", split_axis=0, concat_axis=0, tiled=True)
-    total = lax.all_gather(jnp.sum(pieces, axis=0), "gz", axis=0, tiled=True)
+    total = jnp.broadcast_to(jnp.sum(pieces, axis=0)[None], pieces.shape)
+    total = lax.all_to_all(total, "gz", split_axis=0, concat_axis=0, tiled=True)
     return total.reshape(terms.shape)
 
 
@@ -385,6 +386,13 @@
     after = lax.ppermute(grad_pre[:1], "gz", down)
     grad_planar = jnp.transpose(grad_planar, (1, 0, 2, 3)).reshape(share, planes, modes * modes)
     grad_modes = to_modes(grad_planar, table_z)
+
+    back_terms = jnp.sum(weights32 * grad_modes[None], axis=1).astype(bf16)
+    quarters = lax.all_to_all(back_terms, "col", split_axis=0, concat_axis=0, tiled=True)
+    quarters = quarters.reshape(parts, share, *back_terms.shape[1:])
+    back_modes = jnp.sum(quarters.astype(f32), axis=0)
+    back_slabs = plane_slabs(back_modes, table_z, planes)
+    before, after, back_slabs = lax.optimization_barrier((before, after, back_slabs))
 
     rimmed = jnp.concatenate([before, grad_pre, after], axis=0)
     rimmed = rimmed.reshape((planes + 2) * share, size_x * size_y)
@@ -405,11 +413,6 @@
     grad_conv = sum_over_slabs(products) * scaling
     grad_conv = jnp.transpose(grad_conv.reshape(27, share, channels), (1, 2, 0))
 
-    back_terms = jnp.sum(weights32 * grad_modes[None], axis=1)
-    back_modes = lax.psum_scatter(
-        back_terms.astype(bf16), "col", scatter_dimension=0, tiled=True
-    ).astype(f32)
-    back_slabs = plane_slabs(back_modes, table_z, planes)
     grad_input = final_stage(block, received, back_slabs, tables)
     grad_spectral = spectrum_all[:, None] * grad_modes[None]
     return (layer_out, grad_input, grad_conv, grad_spectral)

time: 242 us -> 179 us (0.74)
  waiting for transfers between devices: 55.8 us -> 16.3 us
  between operations: 14.6 us -> 1.23 us
  starting transfers between devices: 31 us -> 23.8 us
  blocking collectives: 47.6 us -> 42.9 us
  local copies, waits for them, and re-layouts: 32.3 us -> 35.4 us
    all_gather x1 -> x0, blocking collectives: 30.6 us -> none  [sum_over_slabs(): total = lax.all_gather(jnp.sum(pieces, axis=0), 'gz', axis=0, tiled=True)]
    all_to_all x0 -> x3, blocking collectives: none -> 25.9 us  [the longest x1 9.6 us: sum_over_slabs(): lax.all_to_all(terms.reshape(groups, -1), 'gz', split_axis=0, concat_axis...]
    reduce_scatter x1 -> x0, waiting for transfers between devices: 18.4 us -> none  [local(): lax.psum_scatter(back_terms.astype(bf16), 'col', scatter_dimension=0, til...]
    ppermute x1, waiting for transfers between devices: 17.4 us -> 0.01 us  [local(): before = lax.ppermute(grad_pre[planes - 1:], 'gz', up)]
    ppermute x2, waiting for transfers between devices: 0.01 us -> 8.76 us  [halve(): return (mine, lax.ppermute(other, 'col', pairs))]
    all_to_all x2, waiting for transfers between devices: 6.6 us -> 1.05 us  [to_modes(): lax.all_to_all(planes, 'gz', split_axis=2, concat_axis=1, tiled=True)]
    all_to_all x1 -> x0, waiting for transfers between devices: 4.76 us -> none  [sum_over_slabs(): lax.all_to_all(terms.reshape(groups, -1), 'gz', split_axis=0, concat_axis...]
    all_to_all x1 -> x0, starting transfers between devices: 3.99 us -> none  [sum_over_slabs(): lax.all_to_all(terms.reshape(groups, -1), 'gz', split_axis=0, concat_axis...]
  transfers between devices with their start and end apart: 11 -> 9, of which waited for: 6 -> 4; matrix products, arithmetic and copies ran while one was open for 14% -> 18% of each run, Pallas kernels for 5% -> 7%
where the time goes in v3:
time: 179 us; the launch traced here: 178 us
  Pallas kernels  42.9 us (24%)
  blocking collectives  42.9 us (24%)
  local copies, waits for them, and re-layouts  35.4 us (20%)
  starting transfers between devices  23.8 us (13%)
  waiting for transfers between devices  16.3 us (9%)
  other arithmetic  13.4 us (7%)
  matrix products  1.89 us (1%)
    unnamed x48, local copies, waits for them, and re-layouts  16.9 us
    pallas_call x1, Pallas kernels, backward_convs(): pl.pallas_call(partial(back_kernel, rows, size_y, planes), grid=(size_x /...  16.7 us
    pallas_call x1, Pallas kernels, forward_conv(): pl.pallas_call(partial(conv_kernel, rows, size_y), grid=(size_x // rows,)...  12.2 us
    all_to_all x2, starting transfers between devices, to_modes(): lax.all_to_all(planes, 'gz', split_axis=2, concat_axis=1, tiled=True)  10.8 us
    all_to_all x1, blocking collectives, to_slabs(): lax.all_to_all(columns, 'gz', split_axis=1, concat_axis=2, tiled=True)  9.77 us
    all_to_all x1, blocking collectives, sum_over_slabs(): lax.all_to_all(terms.reshape(groups, -1), 'gz', split_axis=0, concat_axis...  9.6 us
    all_to_all x1, blocking collectives, sum_over_slabs(): total = lax.all_to_all(total, 'gz', split_axis=0, concat_axis=0, tiled=True)  9.6 us
    ppermute x2, waiting for transfers between devices, halve(): return (mine, lax.ppermute(other, 'col', pairs))  8.76 us
  transfers between devices with their start and end apart: 9, of which 4 were waited for; matrix products, arithmetic and copies ran while one was open for 18% of the time, Pallas kernels for 7%

profile of v3, /device:TPU:0, one launch (start us, length us, event | category | flops | bytes accessed | tf_op | source)
XLA Modules:
  0.0 177.8 jit_solution(15458561854250186944)
XLA Ops:
  4.0 7.3 %all-to-all-start = ((f32[8,1,1024]{2,1,0:T(1,128)}), f32[8,1,1024]{2,1,0:T(1,128)S(1)}, u32[]{:S(2)}, u32[]{:S(2)}) async-start(f32[8,1,1024]{2,1,0:T(1,128)} %reshape.108), calls=%async_computation | async-start | bytes 65536 | tf_op jit(solution)/shard_map/all_to_all | solution.py:306
  11.3 2.5 %copy.74 = bf16[2,64,128,128]{3,2,1,0:T(8,128)(2,1)S(1)} copy(bf16[2,64,128,128]{3,2,0,1:T(8,128)(2,1)} %bitcast.119) | data formatting | bytes 8388608 | tf_op jit(solution)/shard_map/transpose | solution.py:374
  13.8 5.6 %copy.107 = bf16[16,8,128,128]{3,1,2,0:T(8,128)(2,1)} copy(bf16[16,8,128,128]{3,2,1,0:T(8,128)(2,1)S(1)} %bitcast.117) | data formatting | bytes 8388608
  20.1 12.2 %forward_conv.1 = f32[64,128,128]{2,1,0:T(8,128)S(1)} custom-call(bf16[128,16384]{1,0:T(8,128)(2,1)} %bitcast.113, bf16[128,16384]{1,0:T(8,128)(2,1)} %bitcast.114, bf16[128,16384]{1,0:T(8,128)(2,1)} %bitcast.115, bf16[192,384]{1,0:T(8,128)(2,1)S(1)} %pad_maximum_fusion.2.w_ref), custom_call_target="tpu_custom_call" | custom-call | tf_op jit(solution)/shard_map/forward_conv/pallas_call | solution.py:116
  35.4 2.0 %collective-permute-start = (bf16[16,128,128]{2,1,0:T(8,128)(2,1)}, bf16[16,128,128]{2,1,0:T(8,128)(2,1)S(1)}, u32[]{:S(2)}, u32[]{:S(2)}) collective-permute-start(bf16[16,128,128]{2,1,0:T(8,128)(2,1)} %get-tuple-element.25), channel_id=1, source_target_pairs={{0,4},{4,8},{8,12},{12,16},{16,20},{20,24},{24,28},{28,0},{1,5},{5... | collective-permute-start | bytes 1572872 | tf_op jit(solution)/shard_map/ppermute | solution.py:377
  37.5 2.7 %collective-permute-start.1 = (bf16[16,128,128]{2,1,0:T(8,128)(2,1)}, bf16[16,128,128]{2,1,0:T(8,128)(2,1)S(1)}, u32[]{:S(2)}, u32[]{:S(2)}) collective-permute-start(bf16[16,128,128]{2,1,0:T(8,128)(2,1)} %get-tuple-element.24), channel_id=1, source_target_pairs={{4,0},{8,4},{12,8},{16,12},{20,16},{24,20},{28,24},{0,28},{5,1},{9... | collective-permute-start | bytes 1572872 | tf_op jit(solution)/shard_map/ppermute | solution.py:378
  42.3 7.2 %all_gather.3 = f32[64,16,32]{2,1,0:T(8,128)S(1)} all-gather(f32[16,16,32]{2,1,0:T(8,128)S(1)} %convolution_bitcast_fusion.3), channel_id=1, replica_groups=mesh['gz'=8,'col'=4] {'col'}, dimensions={0}, use_global_device_ids=true | all-gather | bytes 163840 | tf_op jit(solution)/shard_map/all_gather | solution.py:372
  49.8 2.9 %fusion = f32[16,16,32]{2,1,0:T(8,128)S(1)} fusion(bf16[64,16,16,32]{0,3,2,1:T(8,128)(2,1)} %param.12, f32[64,16,32]{0,2,1:T(8,128)S(1)} %copy.79), kind=kLoop, calls=%fused_computation.2 | loop fusion | flops 1564672 | bytes 1212416 | tf_op jit(solution)/shard_map/reduce_sum | solution.py:381
  53.1 9.8 %all_to_all.87 = f32[8,1,1024]{2,1,0:T(1,128)S(1)} all-to-all(f32[8,1,1024]{2,1,0:T(1,128)S(1)} %reshape.110), channel_id=1, replica_groups=mesh['gz'=8,'col'=4] {'gz'}, dimensions={0} | all-to-all | bytes 65536 | tf_op jit(solution)/shard_map/all_to_all | solution.py:312
  64.0 7.9 %gelu_stage.1 = (bf16[16,2,128,128]{3,2,1,0:T(8,128)(2,1)}, bf16[2,16,128,128]{3,2,1,0:T(8,128)(2,1)S(1)}, f32[2,16,16,16]{3,2,1,0:T(8,128)S(1)}) custom-call(f32[4,16,128,128]{3,2,1,0:T(8,128)} %bitcast.103, bf16[16,128,128]{2,1,0:T(8,128)(2,1)S(1)} %collective-permute-done.lo_ref, bf16[16,128,128]{2,1,0:T(8,128)(2,1)S(1)} %collective-permute-done.1.hi_ref, ...), custom_call_target="tpu_custom_call" | custom-call | tf_op jit(solution)/shard_map/gelu_stage/pallas_call | solution.py:164
  76.4 3.5 %all-to-all-start.2 = ((f32[8,1,1024]{2,1,0:T(1,128)}), f32[8,1,1024]{2,1,0:T(1,128)S(1)}, u32[]{:S(2)}, u32[]{:S(2)}) async-start(f32[8,1,1024]{2,1,0:T(1,128)} %reshape.112), calls=%async_computation.2 | async-start | bytes 65536 | tf_op jit(solution)/shard_map/all_to_all | solution.py:306
  82.9 2.8 %collective-permute-start.3 = (bf16[1,16,128,128]{3,2,1,0:T(8,128)(2,1)}, bf16[1,16,128,128]{3,2,1,0:T(8,128)(2,1)}, u32[]{:S(2)}, u32[]{:S(2)}) collective-permute-start(bf16[1,16,128,128]{3,2,1,0:T(8,128)(2,1)} %get-tuple-element.26), channel_id=1, source_target_pairs={{4,0},{8,4},{12,8},{16,12},{20,16},{24,20},{28,24},{0,28},{5,1},{9... | collective-permute-start | bytes 1572872 | tf_op jit(solution)/shard_map/ppermute | solution.py:386
  91.6 3.3 %broadcast_multiply_fusion = (f32[64,16,16,32]{0,3,2,1:T(8,128)}, bf16[64,16,32]{0,2,1:T(8,128)(2,1)}) fusion(f32[16,16,32]{2,1,0:T(8,128)S(1)} %convolution_bitcast_fusion.1, f32[64,16,32]{0,2,1:T(8,128)S(1)} %copy-done.9, bf16[64,16,16,32]{0,3,2,1:T(8,128)(2,1)S(1)} %copy-done.7), kind=kLoop, calls=%fused_computation.11 | loop fusion | flops 2064384 | bytes 3375104 | tf_op jit(solution)/shard_map/mul | solution.py:417
  96.4 6.7 %all_to_all.88 = bf16[4,2,4096]{2,1,0:T(2,128)(2,1)S(1)} all-to-all(bf16[4,2,4096]{2,1,0:T(2,128)(2,1)S(1)} %reshape.114), channel_id=1, replica_groups=mesh['gz'=8,'col'=4] {'col'}, dimensions={0} | all-to-all | bytes 131072 | tf_op jit(solution)/shard_map/all_to_all | solution.py:391
  104.4 3.3 %all-to-all-start.4 = ((f32[8,1,1024]{2,1,0:T(1,128)}), f32[8,1,1024]{2,1,0:T(1,128)S(1)}, u32[]{:S(2)}, u32[]{:S(2)}) async-start(f32[8,1,1024]{2,1,0:T(1,128)} %reshape.116), calls=%async_computation.4 | async-start | bytes 65536 | tf_op jit(solution)/shard_map/all_to_all | solution.py:312
  108.0 6.4 %all-to-all-done.4 = f32[8,1,1024]{2,1,0:T(1,128)S(1)} async-done(((f32[8,1,1024]{2,1,0:T(1,128)}), f32[8,1,1024]{2,1,0:T(1,128)S(1)}, u32[]{:S(2)}, u32[]{:S(2)}) %all-to-all-start.4) | async-done | bytes 32800 | tf_op jit(solution)/shard_map/all_to_all | solution.py:312
  118.2 16.7 %backward_convs.1 = (bf16[128,16384]{1,0:T(8,128)(2,1)}, f32[432,64]{1,0:T(8,128)S(1)}) custom-call(bf16[64,16384]{1,0:T(8,128)(2,1)S(1)} %bitcast.104, bf16[64,16384]{1,0:T(8,128)(2,1)S(1)} %bitcast.105, bf16[64,16384]{1,0:T(8,128)(2,1)S(1)} %bitcast.106, bf16[128,16384]{1,0:T(8,128)(2,1)} %bitcast.116, bf16[128,576]{1,0:T(8,128)(2,1)S(1)} %copy.87.w_ref), custom_call_target="tpu_custom_call" | custom-call | tf_op jit(solution)/shard_map/backward_convs/pallas_call | solution.py:253
  134.9 2.5 %constant_dynamic-slice_fusion.3 = (bf16[2,2,1,16,16384]{4,3,2,1,0:T(8,128)(2,1)S(1)}, bf16[2,2,1,16,16384]{4,3,2,1,0:T(8,128)(2,1)S(1)}) fusion(bf16[2,2,2,16,16384]{4,3,2,1,0:T(8,128)(2,1)} %bitcast.121, s32[]{:T(128)S(6)} %select_n.35, s32[]{:T(128)S(6)} %select_n.36), kind=kLoop, calls=%fused_computation.31 | loop fusion | bytes 8388616 | tf_op jit(solution)/shard_map/jit(dynamic_index_in_dim)/dynamic_slice | solution.py:325
  138.9 4.5 %collective-permute-done.4 = bf16[2,2,16,16384]{3,2,0,1:T(8,128)(2,1)} collective-permute-done((bf16[2,2,16,16384]{3,2,0,1:T(8,128)(2,1)}, bf16[2,2,16,16384]{3,2,0,1:T(8,128)(2,1)}, u32[]{:S(2)}, u32[]{:S(2)}) %collective-permute-start.4) | collective-permute-done | bytes 2097184 | tf_op jit(solution)/shard_map/ppermute | solution.py:327
  143.4 2.1 %fusion.2 = bf16[2,2,16,16384]{3,2,0,1:T(8,128)(2,1)S(1)} fusion(bf16[2,2,16,16384]{3,2,0,1:T(8,128)(2,1)} %collective-permute-done.4, bf16[2,2,1,16,16384]{4,3,2,1,0:T(8,128)(2,1)S(1)} %get-tuple-element.20), kind=kLoop, calls=%fused_computation.6 | loop fusion | flops 4194304 | bytes 6291456 | tf_op jit(solution)/shard_map/convert_element_type | solution.py:405
  146.0 9.6 %all_to_all.89 = f32[8,1,3456]{2,1,0:T(1,128)S(1)} all-to-all(f32[8,1,3456]{2,1,0:T(1,128)S(1)} %all_to_all.79), channel_id=1, replica_groups=mesh['gz'=8,'col'=4] {'gz'}, dimensions={0} | all-to-all | bytes 221184 | tf_op jit(solution)/shard_map/all_to_all | solution.py:332
  155.8 9.6 %all_to_all.90 = f32[8,1,3456]{2,1,0:T(1,128)S(1)} all-to-all(f32[8,1,3456]{2,1,0:T(1,128)S(1)} %broadcast_in_dim.2), channel_id=1, replica_groups=mesh['gz'=8,'col'=4] {'gz'}, dimensions={0} | all-to-all | bytes 221184 | tf_op jit(solution)/shard_map/all_to_all | solution.py:334
  166.7 4.3 %collective-permute-done.5 = bf16[2,1,16,16384]{3,2,0,1:T(8,128)(2,1)} collective-permute-done((bf16[2,1,16,16384]{3,2,0,1:T(8,128)(2,1)S(1)}, bf16[2,1,16,16384]{3,2,0,1:T(8,128)(2,1)}, u32[]{:S(2)}, u32[]{:S(2)}) %collective-permute-start.5) | collective-permute-done | bytes 1048608 | tf_op jit(solution)/shard_map/ppermute | solution.py:327
  172.5 5.3 %final_stage.1 = bf16[16,2,128,128]{3,2,1,0:T(8,128)(2,1)} custom-call(bf16[2,16,128,128]{3,2,1,0:T(8,128)(2,1)S(1)} %bitcast.108, bf16[2,16,128,128]{3,2,1,0:T(8,128)(2,1)S(1)} %bitcast.109, f32[2,16,16,16]{3,2,1,0:T(8,128)S(1)} %bitcast.111, f32[128,16]{1,0:T(8,128)S(1)} %copy-done.2, f32[16,128]{1,0:T(8,128)S(1)} %copy-done.5), custom_call_target="tpu_custom_call" | custom-call | tf_op jit(solution)/shard_map/final_stage/pallas_call | solution.py:288
  (103 shorter events, 35.9 us)
Async XLA Ops:
  0.6 1.4 copy-start.6
  4.0 36.1 %all-to-all-start = ((f32[8,1,1024]{2,1,0:T(1,128)}), f32[8,1,1024]{2,1,0:T(1,128)S(1)}, u32[]{:S(2)}, u32[]{:S(2)}) async-start(f32[8,1,1024]{2,1,0:T(1,128)} %reshape.108), calls=%async_computation | async-start | bytes 65536 | tf_op jit(solution)/shard_map/all_to_all | solution.py:306
  13.8 5.6 %copy-start.12 = (bf16[16,64,27]{1,0,2:T(8,128)(2,1)S(1)}, bf16[16,64,27]{1,0,2:T(8,128)(2,1)}, u32[]{:S(2)}) copy-start(bf16[16,64,27]{1,0,2:T(8,128)(2,1)} %param.11) | copy-start | bytes 165892
  20.0 12.3 %copy-start.10 = (bf16[128,576]{0,1:T(8,128)(2,1)}, bf16[128,576]{0,1:T(8,128)(2,1)S(1)}, u32[]{:S(2)}) copy-start(bf16[128,576]{0,1:T(8,128)(2,1)S(1)} %reshape.85) | copy-start | bytes 442372
  32.3 2.0 %copy-start = (f32[64,128,128]{2,1,0:T(8,128)}, f32[64,128,128]{2,1,0:T(8,128)S(1)}, u32[]{:S(2)}) copy-start(f32[64,128,128]{2,1,0:T(8,128)S(1)} %forward_conv.1) | copy-start | bytes 12582916
  34.4 7.7 %copy-start.15 = (f32[16,16,1]{1,0,2:T(8,128)S(1)}, f32[16,16,1]{1,0,2:T(8,128)}, u32[]{:S(2)}) copy-start(f32[16,16,1]{1,0,2:T(8,128)} %constant.91) | copy-start | bytes 3076
  35.4 28.5 %collective-permute-start = (bf16[16,128,128]{2,1,0:T(8,128)(2,1)}, bf16[16,128,128]{2,1,0:T(8,128)(2,1)S(1)}, u32[]{:S(2)}, u32[]{:S(2)}) collective-permute-start(bf16[16,128,128]{2,1,0:T(8,128)(2,1)} %get-tuple-element.25), channel_id=1, source_target_pairs={{0,4},{4,8},{8,12},{12,16},{16,20},{20,24},{24,28},{28,0},{1,5},{5... | collective-permute-start | bytes 1572872 | tf_op jit(solution)/shard_map/ppermute | solution.py:377
  37.5 26.4 %collective-permute-start.1 = (bf16[16,128,128]{2,1,0:T(8,128)(2,1)}, bf16[16,128,128]{2,1,0:T(8,128)(2,1)S(1)}, u32[]{:S(2)}, u32[]{:S(2)}) collective-permute-start(bf16[16,128,128]{2,1,0:T(8,128)(2,1)} %get-tuple-element.24), channel_id=1, source_target_pairs={{4,0},{8,4},{12,8},{16,12},{20,16},{24,20},{28,24},{0,28},{5,1},{9... | collective-permute-start | bytes 1572872 | tf_op jit(solution)/shard_map/ppermute | solution.py:378
  42.1 10.6 %copy-start.13 = (f32[16,16,1]{0,1,2:T(8,128)S(1)}, f32[16,16,1]{0,1,2:T(8,128)}, u32[]{:S(2)}) copy-start(f32[16,16,1]{0,1,2:T(8,128)} %constant.92) | copy-start | bytes 3076
  49.8 14.1 %copy-start.8 = (f32[64,16,32]{0,2,1:T(8,128)}, f32[64,16,32]{0,2,1:T(8,128)S(1)}, u32[]{:S(2)}) copy-start(f32[64,16,32]{0,2,1:T(8,128)S(1)} %copy.79) | copy-start | bytes 393220
  49.8 14.2 %copy-start.1 = (bf16[16,2,128,128]{3,2,1,0:T(8,128)(2,1)S(1)}, bf16[16,2,128,128]{3,2,1,0:T(8,128)(2,1)}, u32[]{:S(2)}) copy-start(bf16[16,2,128,128]{3,2,1,0:T(8,128)(2,1)} %g_ref.1) | copy-start | bytes 3145732
  49.8 14.2 %copy-start.2 = (f32[128,16]{1,0:T(8,128)S(1)}, f32[128,16]{1,0:T(8,128)}, u32[]{:S(2)}) copy-start(f32[128,16]{1,0:T(8,128)} %constant.77.clone.ext_ref) | copy-start | bytes 24580
  49.8 14.2 %copy-start.5 = (f32[16,128]{1,0:T(8,128)S(1)}, f32[16,128]{1,0:T(8,128)}, u32[]{:S(2)}) copy-start(f32[16,128]{1,0:T(8,128)} %constant.78.clone.ey_ref) | copy-start | bytes 24580
  72.6 17.9 %copy-start.16 = (f32[16,16,1]{1,0,2:T(8,128)S(1)}, f32[16,16,1]{1,0,2:T(8,128)}, u32[]{:S(2)}) copy-start(f32[16,16,1]{1,0,2:T(8,128)} %constant.91) | copy-start | bytes 3076
  72.6 19.0 %copy-start.7 = (bf16[64,16,16,32]{0,3,2,1:T(8,128)(2,1)S(1)}, bf16[64,16,16,32]{0,3,2,1:T(8,128)(2,1)}, u32[]{:S(2)}) copy-start(bf16[64,16,16,32]{0,3,2,1:T(8,128)(2,1)} %param.12) | copy-start | bytes 3145732
  72.6 19.0 %copy-start.9 = (f32[64,16,32]{0,2,1:T(8,128)S(1)}, f32[64,16,32]{0,2,1:T(8,128)}, u32[]{:S(2)}) copy-start(f32[64,16,32]{0,2,1:T(8,128)} %copy-done.8) | copy-start | bytes 393220
  76.4 10.3 %all-to-all-start.2 = ((f32[8,1,1024]{2,1,0:T(1,128)}), f32[8,1,1024]{2,1,0:T(1,128)S(1)}, u32[]{:S(2)}, u32[]{:S(2)}) async-start(f32[8,1,1024]{2,1,0:T(1,128)} %reshape.112), calls=%async_computation.2 | async-start | bytes 65536 | tf_op jit(solution)/shard_map/all_to_all | solution.py:306
  81.0 34.4 %collective-permute-start.2 = (bf16[1,16,128,128]{3,2,1,0:T(8,128)(2,1)}, bf16[1,16,128,128]{3,2,1,0:T(8,128)(2,1)}, u32[]{:S(2)}, u32[]{:S(2)}) collective-permute-start(bf16[1,16,128,128]{3,2,1,0:T(8,128)(2,1)} %get-tuple-element.27), channel_id=1, source_target_pairs={{0,4},{4,8},{8,12},{12,16},{16,20},{20,24},{24,28},{28,0},{1,5},{5... | collective-permute-start | bytes 1572872 | tf_op jit(solution)/shard_map/ppermute | solution.py:385
  82.9 32.5 %collective-permute-start.3 = (bf16[1,16,128,128]{3,2,1,0:T(8,128)(2,1)}, bf16[1,16,128,128]{3,2,1,0:T(8,128)(2,1)}, u32[]{:S(2)}, u32[]{:S(2)}) collective-permute-start(bf16[1,16,128,128]{3,2,1,0:T(8,128)(2,1)} %get-tuple-element.26), channel_id=1, source_target_pairs={{4,0},{8,4},{12,8},{16,12},{20,16},{24,20},{28,24},{0,28},{5,1},{9... | collective-permute-start | bytes 1572872 | tf_op jit(solution)/shard_map/ppermute | solution.py:386
  91.6 11.8 %copy-start.14 = (f32[16,16,1]{0,1,2:T(8,128)S(1)}, f32[16,16,1]{0,1,2:T(8,128)}, u32[]{:S(2)}) copy-start(f32[16,16,1]{0,1,2:T(8,128)} %constant.92) | copy-start | bytes 3076
  94.9 12.8 %copy-start.11 = (bf16[128,576]{0,1:T(8,128)(2,1)S(1)}, bf16[128,576]{0,1:T(8,128)(2,1)}, u32[]{:S(2)}) copy-start(bf16[128,576]{0,1:T(8,128)(2,1)} %copy-done.10) | copy-start | bytes 442372
  104.4 10.0 %all-to-all-start.4 = ((f32[8,1,1024]{2,1,0:T(1,128)}), f32[8,1,1024]{2,1,0:T(1,128)S(1)}, u32[]{:S(2)}, u32[]{:S(2)}) async-start(f32[8,1,1024]{2,1,0:T(1,128)} %reshape.116), calls=%async_computation.4 | async-start | bytes 65536 | tf_op jit(solution)/shard_map/all_to_all | solution.py:312
  138.9 4.5 %collective-permute-start.4 = (bf16[2,2,16,16384]{3,2,0,1:T(8,128)(2,1)}, bf16[2,2,16,16384]{3,2,0,1:T(8,128)(2,1)}, u32[]{:S(2)}, u32[]{:S(2)}) collective-permute-start(bf16[2,2,16,16384]{3,2,0,1:T(8,128)(2,1)} %bitcast.98), channel_id=1, source_target_pairs={{0,1},{1,0},{2,3},{3,2},{4,5},{5,4},{6,7},{7,6},{8,9},{9,8},{10,11... | collective-permute-start | bytes 6291464 | tf_op jit(solution)/shard_map/ppermute | solution.py:327
  145.6 25.4 %collective-permute-start.5 = (bf16[2,1,16,16384]{3,2,0,1:T(8,128)(2,1)S(1)}, bf16[2,1,16,16384]{3,2,0,1:T(8,128)(2,1)}, u32[]{:S(2)}, u32[]{:S(2)}) collective-permute-start(bf16[2,1,16,16384]{3,2,0,1:T(8,128)(2,1)S(1)} %get-tuple-element.22), channel_id=1, source_target_pairs={{0,2},{1,3},{2,0},{3,1},{4,6},{5,7},{6,4},{7,5},{8,10},{9,11},{10,... | collective-permute-start | bytes 3145736 | tf_op jit(solution)/shard_map/ppermute | solution.py:327
  (2 other events, 2.1 us)
